TPU v7x, 128 devices: a whole 4x4x4 slice. The times are simulated.
128 devices in a mesh: ocn: 8 (over z, core), lon: 16 (over y, x).
Axes of the slice: x: 4, y: 4, z: 4, core: 2. Of those that a mesh axis runs over, the one named last changes fastest.
Arguments:
- ocean_state: bfloat16 [4, 12288, 128], P(None, ('ocn', 'lon')), may hold values from -6 to 6
- ice_cover: bfloat16 [12288, 128], P(('ocn', 'lon')), may hold values from 0 to 1
- ice_temp: bfloat16 [12288, 128], P(('ocn', 'lon')), may hold values from -6 to 6
- sea_mask: int32 [12288, 128], P(('ocn', 'lon')), may hold values from 0 to 1
- remap_tiles: bfloat16 [128, 640, 128, 128], P(('ocn', 'lon')), may hold values from 0 to 0.015625
- source_tile: int32 [128, 128, 5], P(('ocn', 'lon')), may hold values from 0 to 95
- send_block: int32 [128, 128, 5], P(('ocn', 'lon')), may hold values from -1 to 49, as said below
- recv_block: int32 [128, 128, 5], P(('ocn', 'lon')), may hold values from -1 to 49, as said below
- atm_state: float32 [4, 6400, 128], P(None, ('ocn', 'lon')), may hold values from -6 to 6
Outputs:
- ocean_fluxes: float32 [6, 12288, 128], P(None, ('ocn', 'lon'))
- atm_fluxes: float32 [6, 6400, 128], P(None, ('ocn', 'lon'))
Inputs may be any that keep to these rules, and one draw needn't show every extreme that they name: `send_block`: -1 marks an empty slot; every slot from a device to itself is filled. recv_block[e, s, c] equals send_block[s, e, c].
All inputs are finite; a program needn't handle non-finite values.
Results may differ from a plain program's by a relative error of at most 0.0019.
Values may be sent and summed in bfloat16 or wider, within the bound.
No kernel may reach another device: no remote copies, remote signals or barrier semaphores. Data moves between devices by JAX's collectives and lax.ppermute only.
A program may use at most 64 MiB of HBM per device.

v0:
```python
import jax
import jax.numpy as jnp
from jax import lax
from jax.sharding import PartitionSpec as P

highest = lax.Precision.HIGHEST


def stack_fields(ocean_state, ice_cover, ice_temp, sea_mask):
    sea_frac = sea_mask.astype(jnp.bfloat16)
    fields = jnp.concatenate([ocean_state, ice_cover[None], ice_temp[None]], 0)
    return jnp.concatenate([fields * sea_frac[None], sea_frac[None]], 0)


def bulk_fluxes(gathered, atm_state):
    inverse = 1.0 / jnp.maximum(gathered[6], 0.1)
    surface_temp = gathered[0] * inverse
    current_u = gathered[1] * inverse
    current_v = gathered[2] * inverse
    salinity = gathered[3] * inverse
    ice_frac = gathered[4] * inverse
    ice_surface = gathered[5] * inverse
    slip_east = atm_state[0] - current_u
    slip_north = atm_state[1] - current_v
    wind_speed = jnp.sqrt(slip_east * slip_east + slip_north * slip_north + 0.25)
    open_water = 1.0 - ice_frac
    saturation = 0.5 * jnp.exp(0.2 * surface_temp) * (1.0 - 0.05 * salinity)
    evaporation = 0.3 * open_water * wind_speed * (saturation - atm_state[3])
    heat = (
        0.3
        * wind_speed
        * (open_water * (surface_temp - atm_state[2]) + ice_frac * (ice_surface - atm_state[2]))
        + 2.5 * evaporation
    )
    return jnp.stack(
        [
            0.5 * open_water * wind_speed * slip_east,
            0.5 * open_water * wind_speed * slip_north,
            0.8 * ice_frac * wind_speed * slip_east,
            0.8 * ice_frac * wind_speed * slip_north,
            heat,
            evaporation,
        ],
        0,
    )


def shards(
    ocean_state,
    ice_cover,
    ice_temp,
    sea_mask,
    remap_tiles,
    source_tile,
    send_block,
    recv_block,
    atm_state,
):
    rows_ocn = lax.axis_size("ocn")
    rows_lon = lax.axis_size("lon")
    peers = rows_ocn * rows_lon
    slots = remap_tiles.shape[1]
    capacity = slots // peers
    width = sea_mask.shape[1]
    ocean_tiles = sea_mask.shape[0]
    atm_tiles = atm_state.shape[1]
    tiles = remap_tiles[0]
    sources = source_tile[0].reshape(slots)
    targets = send_block[0].reshape(slots)
    filled = (targets >= 0).astype(jnp.float32)
    stacked = stack_fields(ocean_state, ice_cover, ice_temp, sea_mask)
    picked = jnp.take(stacked, sources, axis=1)
    contrib = jnp.einsum("fsi,sij->sfj", picked, tiles, preferred_element_type=jnp.float32)
    contrib = (contrib * filled[:, None, None]).astype(jnp.bfloat16)
    arriving = lax.all_to_all(
        contrib.reshape(peers, capacity, 7, width),
        ("ocn", "lon"),
        split_axis=0,
        concat_axis=0,
        tiled=True,
    )
    arriving = arriving.reshape(slots, 7, width)
    blocks = recv_block[0].reshape(slots)
    onehot = (blocks[None, :] == jnp.arange(atm_tiles, dtype=jnp.int32)[:, None]).astype(
        jnp.float32
    )
    gathered = jnp.einsum("bs,sfj->fbj", onehot, arriving.astype(jnp.float32), precision=highest)
    fluxes = bulk_fluxes(gathered, atm_state)
    back = jnp.einsum("bs,fbj->sfj", onehot, fluxes, precision=highest).astype(jnp.bfloat16)
    returning = lax.all_to_all(
        back.reshape(peers, capacity, 6, width),
        ("ocn", "lon"),
        split_axis=0,
        concat_axis=0,
        tiled=True,
    )
    returning = returning.reshape(slots, 6, width)
    owners = (sources[None, :] == jnp.arange(ocean_tiles, dtype=jnp.int32)[:, None]).astype(
        jnp.float32
    ) * filled[None, :]
    terms = jnp.einsum("sfj,sij->sfi", returning, tiles, preferred_element_type=jnp.float32)
    ones_column = jnp.ones((width,), jnp.bfloat16)
    coverage = jnp.einsum("sij,j->si", tiles, ones_column, preferred_element_type=jnp.float32)
    summed = jnp.einsum("bs,sfi->fbi", owners, terms, precision=highest)
    cover = jnp.dot(owners, coverage, precision=highest)
    ocean_fluxes = summed / jnp.maximum(cover, 0.1)[None] * sea_mask.astype(jnp.float32)[None]
    return (ocean_fluxes, fluxes)


def solution(mesh):
    in_specs = (
        P(None, ("ocn", "lon"), None),
        P(("ocn", "lon"), None),
        P(("ocn", "lon"), None),
        P(("ocn", "lon"), None),
        P(("ocn", "lon"), None, None, None),
        P(("ocn", "lon"), None, None),
        P(("ocn", "lon"), None, None),
        P(("ocn", "lon"), None, None),
        P(None, ("ocn", "lon"), None),
    )
    out_specs = (P(None, ("ocn", "lon"), None), P(None, ("ocn", "lon"), None))
    return jax.shard_map(shards, mesh=mesh, in_specs=in_specs, out_specs=out_specs, check_vma=False)
```

profile of v0, /device:TPU:1, one launch (start us, length us, event | category | flops | bytes accessed | tf_op | source)
XLA Modules:
  0.0 100.5 jit_solution(4548497070739469924)
XLA Ops:
  0.6 0.8 copy.29
  1.4 0.2 reshape_squeeze.7
  1.6 0.2 reshape_squeeze.6
  1.8 0.9 fusion.60
  2.7 0.9 copy.30
  3.7 0.8 copy.31
  4.5 0.8 copy.32
  5.3 0.7 compare_convert_fusion
  6.1 0.2 reshape.75
  6.3 0.2 maximum_multiply_fusion
  6.7 2.4 %gather_fusion = bf16[640,7,128]{2,1,0:T(8,128)(2,1)S(1)} fusion(bf16[7,96,128]{2,0,1:T(8,128)(2,1)S(1)} %pad_maximum_fusion, s32[1024]{0:T(1024)S(1)} %pad_clamp_fusion), kind=kCustom, calls=%fused_computation | custom fusion | bytes 2296320 | tf_op jit(solution)/shard_map/jit(_take)/gather | solution.py:72
  9.0 12.5 %multiply_convert_fusion = bf16[640,7,128]{2,1,0:T(8,128)(2,1)} fusion(bf16[1,640,128,128]{3,2,1,0:T(8,128)(2,1)} %param.13, bf16[640,7,128]{2,1,0:T(8,128)(2,1)S(1)} %gather_fusion, f32[640]{0:T(1024)S(1)} %reshape.75, pred[640]{0:T(1024)(128)(4,1)S(1)} %compare_and_fusion), kind=kOutput, calls=%fused_computation.7 | convolution fusion | flops 148520960 | bytes 23268480 | tf_op jit(solution)/shard_map/fsi,sij->sfj/dot_general | solution.py:73
  21.5 11.5 %all-to-all-start = ((bf16[128,5,7,128]{3,2,1,0:T(8,128)(2,1)}), bf16[128,5,7,128]{3,2,1,0:T(8,128)(2,1)S(1)}, u32[]{:S(2)}, u32[]{:S(2)}) async-start(bf16[128,5,7,128]{3,2,1,0:T(8,128)(2,1)} %bitcast.6), calls=%async_computation | async-start | bytes 2621440 | tf_op jit(solution)/shard_map/all_to_all | solution.py:75
  33.1 0.2 eq.28
  33.4 21.1 %all-to-all-done = bf16[128,5,7,128]{3,2,1,0:T(8,128)(2,1)S(1)} async-done(((bf16[128,5,7,128]{3,2,1,0:T(8,128)(2,1)}), bf16[128,5,7,128]{3,2,1,0:T(8,128)(2,1)S(1)}, u32[]{:S(2)}, u32[]{:S(2)}) %all-to-all-start) | async-done | bytes 1146912 | tf_op jit(solution)/shard_map/all_to_all | solution.py:75
  54.5 0.3 convolution_bitcast_fusion
  55.0 1.0 convolution_convert_fusion
  56.0 1.8 %copy.41 = bf16[640,6,128]{2,1,0:T(8,128)(2,1)} copy(bf16[640,6,128]{2,0,1:T(8,128)(2,1)S(1)} %convolution_convert_fusion) | data formatting | bytes 1966080 | tf_op jit(solution)/shard_map/convert_element_type | solution.py:89
  57.7 4.8 %all-to-all-start.1 = ((bf16[128,5,6,128]{3,2,1,0:T(8,128)(2,1)}), bf16[128,5,6,128]{3,2,1,0:T(8,128)(2,1)S(1)}, u32[]{:S(2)}, u32[]{:S(2)}) async-start(bf16[128,5,6,128]{3,2,1,0:T(8,128)(2,1)} %bitcast.9), calls=%async_computation.1 | async-start | bytes 2621440 | tf_op jit(solution)/shard_map/all_to_all | solution.py:90
  62.5 9.8 %fusion = f32[1,640,128]{2,0,1:T(1,128)S(1)} fusion(bf16[1,640,128,128]{3,2,1,0:T(8,128)(2,1)} %param.13), kind=kOutput, calls=%fused_computation.1 | convolution fusion | flops 20971520 | bytes 21299200 | tf_op jit(solution)/shard_map/sij,j->si/dot_general | solution.py:103
  72.3 0.4 convolution_maximum_fusion
  72.7 11.4 %all-to-all-done.1 = bf16[128,5,6,128]{3,2,1,0:T(8,128)(2,1)S(1)} async-done(((bf16[128,5,6,128]{3,2,1,0:T(8,128)(2,1)}), bf16[128,5,6,128]{3,2,1,0:T(8,128)(2,1)S(1)}, u32[]{:S(2)}, u32[]{:S(2)}) %all-to-all-start.1) | async-done | bytes 983072 | tf_op jit(solution)/shard_map/all_to_all | solution.py:90
  84.1 14.1 %fusion.2 = f32[640,6,128]{2,1,0:T(8,128)S(1)} fusion(bf16[640,6,128]{2,1,0:T(8,128)(2,1)S(1)} %bitcast.39, bf16[1,640,128,128]{3,2,1,0:T(8,128)(2,1)} %param.13), kind=kOutput, calls=%fused_computation.3 | convolution fusion | flops 125829120 | bytes 23920640 | tf_op jit(solution)/shard_map/sfj,sij->sfi/dot_general | solution.py:101
  98.3 2.2 %fusion.19 = f32[6,96,128]{2,1,0:T(8,128)} fusion(f32[640,6,128]{2,1,0:T(8,128)S(1)} %fusion.2, f32[96,128]{1,0:T(8,128)S(1)} %get-tuple-element.10, f32[96,128]{1,0:T(8,128)S(1)} %convolution_maximum_fusion, f32[640]{0:T(1024)S(1)} %reshape.75, s32[640]{0:T(1024)S(1)} %reshape_squeeze.6), kind=kOutput, calls=%fused_computation.16 | convolution fusion | flops 566501376 | bytes 2364416 | tf_op jit(solution)/shard_map/bs,sfi->fbi/dot_general | solution.py:104
  (20 shorter events, 0.7 us)
Async XLA Ops:
  21.5 11.5 %copy-start.2 = (s32[1,128,5]{1,0,2:T(1,128)S(1)}, s32[1,128,5]{1,0,2:T(1,128)}, u32[]{:S(2)}) copy-start(s32[1,128,5]{1,0,2:T(1,128)} %param.16) | copy-start | bytes 7684
  21.5 11.8 %copy-start.1 = (f32[4,50,128]{2,0,1:T(4,128)S(1)}, f32[4,50,128]{2,0,1:T(4,128)}, u32[]{:S(2)}) copy-start(f32[4,50,128]{2,0,1:T(4,128)} %param.17) | copy-start | bytes 307204
  21.5 33.0 %all-to-all-start = ((bf16[128,5,7,128]{3,2,1,0:T(8,128)(2,1)}), bf16[128,5,7,128]{3,2,1,0:T(8,128)(2,1)S(1)}, u32[]{:S(2)}, u32[]{:S(2)}) async-start(bf16[128,5,7,128]{3,2,1,0:T(8,128)(2,1)} %bitcast.6), calls=%async_computation | async-start | bytes 2621440 | tf_op jit(solution)/shard_map/all_to_all | solution.py:75
  55.0 2.7 %copy-start = (f32[6,50,128]{2,1,0:T(8,128)}, f32[6,50,128]{2,1,0:T(8,128)S(1)}, u32[]{:S(2)}) copy-start(f32[6,50,128]{2,1,0:T(8,128)S(1)} %fusion.50) | copy-start | bytes 460804
  57.7 26.4 %all-to-all-start.1 = ((bf16[128,5,6,128]{3,2,1,0:T(8,128)(2,1)}), bf16[128,5,6,128]{3,2,1,0:T(8,128)(2,1)S(1)}, u32[]{:S(2)}, u32[]{:S(2)}) async-start(bf16[128,5,6,128]{3,2,1,0:T(8,128)(2,1)} %bitcast.9), calls=%async_computation.1 | async-start | bytes 2621440 | tf_op jit(solution)/shard_map/all_to_all | solution.py:90
where the time goes:
time: 101 us; the launch traced here: 100 us
  matrix products  40.2 us (40%)
  waiting for transfers between devices  32.5 us (32%)
  starting transfers between devices  16.3 us (16%)
  local copies, waits for them, and re-layouts  8.57 us (8%)
  other arithmetic  2.11 us (2%)
    all_to_all x1, waiting for transfers between devices, shards(): lax.all_to_all(contrib.reshape(peers, capacity, 7, width), ('ocn', 'lon')...  21.1 us
    dot_general x1, matrix products, shards(): jnp.einsum('sfj,sij->sfi', returning, tiles, preferred_element_type=jnp.f...  14.1 us
    dot_general x1, matrix products, shards(): jnp.einsum('fsi,sij->sfj', picked, tiles, preferred_element_type=jnp.floa...  12.5 us
    all_to_all x1, starting transfers between devices, shards(): lax.all_to_all(contrib.reshape(peers, capacity, 7, width), ('ocn', 'lon')...  11.5 us
    all_to_all x1, waiting for transfers between devices, shards(): lax.all_to_all(back.reshape(peers, capacity, 6, width), ('ocn', 'lon'), s...  11.4 us
    dot_general x1, matrix products, shards(): jnp.einsum('sij,j->si', tiles, ones_column, preferred_element_type=jnp.fl...  9.77 us
    all_to_all x1, starting transfers between devices, shards(): lax.all_to_all(back.reshape(peers, capacity, 6, width), ('ocn', 'lon'), s...  4.77 us
    gather x1, local copies, waits for them, and re-layouts, shards(): picked = jnp.take(stacked, sources, axis=1)  2.36 us
  transfers between devices with their start and end apart: 2, of which 2 were waited for; matrix products, arithmetic and copies ran while one was open for 11% of the time, Pallas kernels for 0%

commit v1 on v0

v1 whole, which is shorter than its diff:
```python
import jax
import jax.numpy as jnp
from jax import lax
from jax.experimental import pallas as pl
from jax.experimental.pallas import tpu as pltpu
from jax.sharding import PartitionSpec as P

AXES = ("ocn", "lon")
MB = 1024 * 1024

PEER_BIT = 10
TILE_BIT = 18
GROUP = 16
CHUNKS = 16
SUMS = 4


def code_parts(code):
    slot = code & ((1 << PEER_BIT) - 1)
    peer = (code >> PEER_BIT) & ((1 << (TILE_BIT - PEER_BIT)) - 1)
    return slot, peer, code >> TILE_BIT


def forward_kernel(
    state_hbm,
    cover_hbm,
    temp_hbm,
    mask_hbm,
    tiles_hbm,
    source_hbm,
    target_hbm,
    kept,
    wire,
    listed,
    state,
    cover,
    temp,
    mask,
    source,
    target,
    fields,
    rows,
    sems,
    tile_sems,
):
    capacity, _, peers = target.shape
    slots = kept.shape[0]
    ocean_tiles = mask.shape[0]
    per_chunk = slots // CHUNKS
    peers_chunk = peers // CHUNKS
    wire_rows = wire.shape[0]
    small = (
        (source_hbm, source),
        (target_hbm, target),
        (mask_hbm, mask),
        (state_hbm, state),
        (cover_hbm, cover),
        (temp_hbm, temp),
    )
    copies = [pltpu.make_async_copy(a, b, sems.at[i]) for i, (a, b) in enumerate(small)]
    for copy in copies:
        copy.start()

    def chunk_copy(k):
        part = pl.ds(k * per_chunk, per_chunk)
        return pltpu.make_async_copy(tiles_hbm.at[part], kept.at[part], tile_sems.at[k])

    for k in range(CHUNKS):
        chunk_copy(k).start()
    for copy in copies:
        copy.wait()

    sea = mask[...].astype(jnp.float32)
    for f in range(4):
        fields[pl.ds(f, ocean_tiles, stride=8), :] = state[f].astype(jnp.float32) * sea
    fields[pl.ds(4, ocean_tiles, stride=8), :] = cover[...].astype(jnp.float32) * sea
    fields[pl.ds(5, ocean_tiles, stride=8), :] = temp[...].astype(jnp.float32) * sea
    fields[pl.ds(6, ocean_tiles, stride=8), :] = sea
    fields[pl.ds(7, ocean_tiles, stride=8), :] = jnp.zeros_like(sea)
    fields[8 * ocean_tiles :, :] = jnp.zeros((8, sea.shape[1]), jnp.float32)

    def list_peer(p, count):
        for c in range(capacity):
            tile = source[c, 0, p]
            listed[count] = (p * (capacity + (1 << PEER_BIT)) + c) + (tile << TILE_BIT)
            count = count + (target[c, 0, p] >= 0).astype(jnp.int32)
        return count

    count = lax.fori_loop(0, peers, list_peer, jnp.int32(0), unroll=4)
    spare = (slots - 1) + ((wire_rows - 7 * (slots - 1)) << PEER_BIT) + (ocean_tiles << TILE_BIT)
    for k in range(GROUP):
        listed[count + k] = spare
    groups = (count + (GROUP - 1)) // GROUP
    listed[slots + GROUP] = groups

    def wait_chunk(k, carry):
        chunk_copy(k).wait()
        return carry

    def group(g, waited):
        parts = [code_parts(listed[g * GROUP + k]) for k in range(GROUP)]
        need = jnp.minimum(parts[-1][1] // peers_chunk + 1, CHUNKS)
        lax.fori_loop(waited, need, wait_chunk, 0)
        for k in range(0, GROUP, 2):
            (s0, p0, t0), (s1, p1, t1) = parts[k], parts[k + 1]
            left = jnp.concatenate(
                [
                    fields[pl.ds(pl.multiple_of(t0 * 8, 8), 8), :],
                    fields[pl.ds(pl.multiple_of(t1 * 8, 8), 8), :],
                ],
                0,
            ).astype(jnp.bfloat16)
            right = jnp.concatenate([kept[s0], kept[s1]], 1)
            out = jnp.dot(left, right, preferred_element_type=jnp.float32)
            rows[pl.ds(7 * s0 + p0, 7), :] = out[0:7, 0:128]
            rows[pl.ds(7 * s1 + p1, 7), :] = out[8:15, 128:256]
        return jnp.maximum(waited, need)

    waited = lax.fori_loop(0, groups, group, jnp.int32(0))
    lax.fori_loop(waited, CHUNKS, wait_chunk, 0)
    step = wire_rows // 18

    def round_rows(i, carry):
        part = pl.ds(pl.multiple_of(i * step, 16), step)
        wire[part, :] = rows[part, :].astype(jnp.bfloat16)
        return carry

    lax.fori_loop(0, 18, round_rows, 0)


def atmosphere_kernel(
    arrived, block_hbm, state, fluxes, wire, block, wide, sums, table, out_rows, sem
):
    capacity, _, peers = block.shape
    atm_tiles = state.shape[0]
    copy = pltpu.make_async_copy(block_hbm, block, sem)
    copy.start()
    in_rows = arrived.shape[0]
    step = in_rows // 18

    def widen(i, carry):
        part = pl.ds(pl.multiple_of(i * step, 16), step)
        wide[part, :] = arrived[part, :].astype(jnp.float32)
        return carry

    lax.fori_loop(0, 18, widen, 0)
    for c in range(capacity):
        sums[c] = jnp.zeros(sums.shape[1:], jnp.float32)
    copy.wait()

    def tile_of(p, c):
        b = block[c, 0, p]
        return pl.multiple_of(jnp.where(b < 0, atm_tiles, b) * 8, 8)

    def gather(p, carry):
        for c in range(capacity):
            part = pl.ds(tile_of(p, c), 8)
            sums[c, part, :] = sums[c, part, :] + wide[pl.ds(p * 36 + c * 7, 8), :]
        return carry

    lax.fori_loop(0, peers, gather, 0, unroll=4)
    gathered = []
    for f in range(7):
        part = pl.ds(f, atm_tiles, stride=8)
        total = sums[0, part, :]
        for c in range(1, capacity):
            total = total + sums[c, part, :]
        gathered.append(total)
    inverse = 1.0 / jnp.maximum(gathered[6], 0.1)
    surface_temp, current_u, current_v, salinity, ice_frac, ice_surface = [
        g * inverse for g in gathered[:6]
    ]
    wind_u, wind_v, air_temp, humidity = [state[:, k, :] for k in range(4)]
    slip_east = wind_u - current_u
    slip_north = wind_v - current_v
    speed = jnp.sqrt(slip_east * slip_east + slip_north * slip_north + 0.25)
    open_water = 1.0 - ice_frac
    saturation = 0.5 * jnp.exp(0.2 * surface_temp) * (1.0 - 0.05 * salinity)
    evaporation = 0.3 * open_water * speed * (saturation - humidity)
    heat = (
        0.3
        * speed
        * (open_water * (surface_temp - air_temp) + ice_frac * (ice_surface - air_temp))
        + 2.5 * evaporation
    )
    results = (
        0.5 * open_water * speed * slip_east,
        0.5 * open_water * speed * slip_north,
        0.8 * ice_frac * speed * slip_east,
        0.8 * ice_frac * speed * slip_north,
        heat,
        evaporation,
    )
    for f, value in enumerate(results):
        fluxes[f] = value
        table[pl.ds(f, atm_tiles, stride=8), :] = value
    table[8 * atm_tiles :, :] = jnp.zeros((8, value.shape[1]), jnp.float32)

    def send(p, carry):
        for c in range(capacity):
            out_rows[pl.ds(p * 30 + c * 6, 6), :] = table[pl.ds(tile_of(p, c), 6), :]
        return carry

    lax.fori_loop(0, peers, send, 0, unroll=4)
    back_step = wire.shape[0] // 16

    def round_rows(i, carry):
        part = pl.ds(pl.multiple_of(i * back_step, 16), back_step)
        wire[part, :] = out_rows[part, :].astype(jnp.bfloat16)
        return carry

    lax.fori_loop(0, 16, round_rows, 0)


def ocean_kernel(returned, kept, list_hbm, mask, out, listed, wide, sums, sem):
    slots = kept.shape[0]
    ocean_tiles = mask.shape[0]
    copy = pltpu.make_async_copy(list_hbm, listed, sem)
    copy.start()
    in_rows = returned.shape[0]
    step = in_rows // 16

    def widen(i, carry):
        part = pl.ds(pl.multiple_of(i * step, 16), step)
        wide[part, :] = returned[part, :].astype(jnp.float32)
        return carry

    lax.fori_loop(0, 16, widen, 0)
    wide[in_rows:, :] = jnp.zeros((8, wide.shape[1]), jnp.float32)
    for k in range(SUMS):
        sums[k] = jnp.zeros(sums.shape[1:], jnp.float32)
    copy.wait()
    row = lax.broadcasted_iota(jnp.int32, (8, 128), 0)

    def group(g, carry):
        parts = [code_parts(listed[g * GROUP + k]) for k in range(GROUP)]
        for k in range(0, GROUP, 2):
            left = []
            for slot, _, _ in parts[k : k + 2]:
                values = wide[pl.ds(6 * slot, 8), :]
                left.append(jnp.where(row < 6, values, jnp.where(row == 6, 1.0, 0.0)))
            left = jnp.concatenate(left, 0).astype(jnp.bfloat16)
            right = jnp.concatenate([kept[parts[k][0]], kept[parts[k + 1][0]]], 0)
            terms = lax.dot_general(
                left, right, (((1,), (1,)), ((), ())), preferred_element_type=jnp.float32
            )
            for j in range(2):
                tile = parts[k + j][2]
                part = pl.ds(pl.multiple_of(tile * 8, 8), 8)
                n = (k + j) % SUMS
                sums[n, part, :] = (
                    sums[n, part, :] + terms[8 * j : 8 * j + 8, 128 * j : 128 * j + 128]
                )
        return carry

    lax.fori_loop(0, listed[slots + GROUP], group, 0)

    def total(f):
        part = pl.ds(f, ocean_tiles, stride=8)
        value = sums[0, part, :]
        for k in range(1, SUMS):
            value = value + sums[k, part, :]
        return value

    scale = mask[...].astype(jnp.float32) / jnp.maximum(total(6), 0.1)
    for f in range(6):
        out[f] = total(f) * scale


def anywhere():
    return pl.BlockSpec(memory_space=pl.ANY)


def in_vmem():
    return pl.BlockSpec(memory_space=pltpu.VMEM)


def exchange(rows, peers):
    wire = rows.reshape(peers, rows.shape[0] // (2 * peers), 2, rows.shape[1])
    arrived = lax.all_to_all(wire, AXES, split_axis=0, concat_axis=0, tiled=True)
    return arrived.reshape(rows.shape)


def shards(
    ocean_state,
    ice_cover,
    ice_temp,
    sea_mask,
    remap_tiles,
    source_tile,
    send_block,
    recv_block,
    atm_state,
):
    peers, capacity = send_block.shape[1:]
    slots = peers * capacity
    ocean_tiles, width = sea_mask.shape
    atm_tiles = atm_state.shape[1]
    source = source_tile.transpose(2, 0, 1)
    target = send_block.transpose(2, 0, 1)
    block = recv_block.transpose(2, 0, 1)
    list_size = slots + GROUP + 16
    kept, wire, listed = pl.pallas_call(
        forward_kernel,
        in_specs=[anywhere()] * 7,
        out_specs=[in_vmem(), in_vmem(), pl.BlockSpec(memory_space=pltpu.SMEM)],
        out_shape=[
            pltpu.VMEM((slots, width, width), jnp.bfloat16),
            jax.ShapeDtypeStruct((36 * peers, width), jnp.bfloat16),
            jax.ShapeDtypeStruct((list_size,), jnp.int32),
        ],
        scratch_shapes=[
            pltpu.VMEM(ocean_state.shape, jnp.bfloat16),
            pltpu.VMEM(ice_cover.shape, jnp.bfloat16),
            pltpu.VMEM(ice_temp.shape, jnp.bfloat16),
            pltpu.VMEM(sea_mask.shape, jnp.int32),
            pltpu.SMEM(source.shape, jnp.int32),
            pltpu.SMEM(target.shape, jnp.int32),
            pltpu.VMEM((8 * (ocean_tiles + 1), width), jnp.float32),
            pltpu.VMEM((36 * peers + 8, width), jnp.float32),
            pltpu.SemaphoreType.DMA((6,)),
            pltpu.SemaphoreType.DMA((CHUNKS,)),
        ],
        compiler_params=pltpu.CompilerParams(vmem_limit_bytes=16 * MB),
        name="forward",
    )(ocean_state, ice_cover, ice_temp, sea_mask, remap_tiles[0], source, target)
    arrived = exchange(wire, peers)
    fluxes, wire_back = pl.pallas_call(
        atmosphere_kernel,
        in_specs=[in_vmem(), anywhere(), in_vmem()],
        out_specs=[in_vmem(), in_vmem()],
        out_shape=[
            jax.ShapeDtypeStruct((6, atm_tiles, width), jnp.float32),
            jax.ShapeDtypeStruct((30 * peers, width), jnp.bfloat16),
        ],
        scratch_shapes=[
            pltpu.SMEM(block.shape, jnp.int32),
            pltpu.VMEM((36 * peers + 8, width), jnp.float32),
            pltpu.VMEM((capacity, 8 * (atm_tiles + 1), width), jnp.float32),
            pltpu.VMEM((8 * (atm_tiles + 1), width), jnp.float32),
            pltpu.VMEM((30 * peers, width), jnp.float32),
            pltpu.SemaphoreType.DMA,
        ],
        compiler_params=pltpu.CompilerParams(vmem_limit_bytes=16 * MB),
        name="atmosphere",
    )(arrived, block, atm_state.transpose(1, 0, 2))
    returned = exchange(wire_back, peers)
    ocean_fluxes = pl.pallas_call(
        ocean_kernel,
        in_specs=[in_vmem(), in_vmem(), anywhere(), in_vmem()],
        out_specs=in_vmem(),
        out_shape=jax.ShapeDtypeStruct((6, ocean_tiles, width), jnp.float32),
        scratch_shapes=[
            pltpu.SMEM((list_size,), jnp.int32),
            pltpu.VMEM((30 * peers + 8, width), jnp.float32),
            pltpu.VMEM((SUMS, 8 * (ocean_tiles + 1), width), jnp.float32),
            pltpu.SemaphoreType.DMA,
        ],
        compiler_params=pltpu.CompilerParams(vmem_limit_bytes=16 * MB),
        name="ocean",
    )(returned, kept, listed, sea_mask)
    return (ocean_fluxes, fluxes)


def solution(mesh):
    in_specs = (
        P(None, AXES, None),
        P(AXES, None),
        P(AXES, None),
        P(AXES, None),
        P(AXES, None, None, None),
        P(AXES, None, None),
        P(AXES, None, None),
        P(AXES, None, None),
        P(None, AXES, None),
    )
    out_specs = (P(None, AXES, None), P(None, AXES, None))
    return jax.shard_map(shards, mesh=mesh, in_specs=in_specs, out_specs=out_specs, check_vma=False)
```

time: 101 us -> 80.9 us (0.80)
  blocking collectives: 0 us -> 53.8 us
  matrix products: 40.2 us -> 0 us
  waiting for transfers between devices: 32.5 us -> 0 us
  Pallas kernels: 0 us -> 21.4 us
  starting transfers between devices: 16.3 us -> 0 us
  local copies, waits for them, and re-layouts: 8.57 us -> 4.54 us
  other arithmetic: 2.11 us -> 0 us
    all_to_all x0 -> x2, blocking collectives: none -> 53.8 us  [exchange(): lax.all_to_all(wire, AXES, split_axis=0, concat_axis=0, tiled=True)]
    dot_general x7 -> x0, matrix products: 40.2 us -> none  [the longest x1 14.1 us: shards(): jnp.einsum('sfj,sij->sfi', returning, tiles, preferred_element_type=jnp.f...]
    all_to_all x2 -> x0, waiting for transfers between devices: 32.5 us -> none  [the longest x1 21.1 us: shards(): lax.all_to_all(contrib.reshape(peers, capacity, 7, width), ('ocn', 'lon')...]
    pallas_call x0 -> x3, Pallas kernels: none -> 21.4 us  [the longest x1 9.05 us: shards(): pl.pallas_call(forward_kernel, in_specs=[anywhere()] * 7, out_specs=[in_v...]
    all_to_all x2 -> x0, starting transfers between devices: 16.3 us -> none  [the longest x1 11.5 us: shards(): lax.all_to_all(contrib.reshape(peers, capacity, 7, width), ('ocn', 'lon')...]
    unnamed x9 -> x18, local copies, waits for them, and re-layouts: 1.86 us -> 4.54 us
    gather x1 -> x0, local copies, waits for them, and re-layouts: 2.36 us -> none  [shards(): picked = jnp.take(stacked, sources, axis=1)]
    convert_element_type x3 -> x0, local copies, waits for them, and re-layouts: 2.07 us -> none  [the longest x1 1.75 us: shards(): jnp.einsum('bs,fbj->sfj', onehot, fluxes, precision=highest)]
  transfers between devices with their start and end apart: 2 -> 0, of which waited for: 2 -> 0; matrix products, arithmetic and copies ran while one was open for 11% -> 0% of each run, Pallas kernels for 0% -> 0%
where the time goes in v1:
time: 80.9 us; the launch traced here: 80.5 us
  blocking collectives  53.8 us (67%)
  Pallas kernels  21.4 us (26%)
  local copies, waits for them, and re-layouts  4.54 us (6%)
    all_to_all x2, blocking collectives, exchange(): lax.all_to_all(wire, AXES, split_axis=0, concat_axis=0, tiled=True)  53.8 us
    pallas_call x1, Pallas kernels, shards(): pl.pallas_call(forward_kernel, in_specs=[anywhere()] * 7, out_specs=[in_v...  9.05 us
    pallas_call x1, Pallas kernels, shards(): pl.pallas_call(ocean_kernel, in_specs=[in_vmem(), in_vmem(), anywhere(),...  6.54 us
    pallas_call x1, Pallas kernels, shards(): pl.pallas_call(atmosphere_kernel, in_specs=[in_vmem(), anywhere(), in_vme...  5.84 us
    unnamed x18, local copies, waits for them, and re-layouts  4.54 us

profile of v1, /device:TPU:1, one launch (start us, length us, event | category | flops | bytes accessed | tf_op | source)
XLA Modules:
  0.0 80.5 jit_solution(11316295297380336994)
XLA Ops:
  0.6 0.0 copy-start.8
  0.6 0.0 copy-start
  0.7 0.8 copy-done
  1.4 0.0 copy-start.3
  1.5 0.9 %copy-done.3 = bf16[4,96,128]{2,1,0:T(8,128)(2,1)S(1)} copy-done((bf16[4,96,128]{2,1,0:T(8,128)(2,1)S(1)}, bf16[4,96,128]{2,1,0:T(8,128)(2,1)}, u32[]{:S(2)}) %copy-start.3) | copy-done | bytes 98328
  2.3 0.0 copy-start.4
  2.3 0.7 copy-done.4
  3.1 0.0 copy-start.5
  3.1 0.7 copy-done.5
  3.8 0.0 copy-start.6
  3.8 0.7 copy-done.6
  4.5 0.0 copy-start.7
  4.5 0.7 copy-done.7
  5.2 0.0 copy-start.2
  5.2 0.0 copy-start.1
  5.2 9.1 %forward.1 = (bf16[640,128,128]{2,1,0:T(8,128)(2,1)S(1)}, bf16[4608,128]{1,0:T(8,128)(2,1)S(1)}, s32[672]{0:T(1024)S(1)}) custom-call(bf16[4,96,128]{2,1,0:T(8,128)(2,1)S(1)} %copy-done.3, bf16[96,128]{1,0:T(8,128)(2,1)S(1)} %copy-done.4, bf16[96,128]{1,0:T(8,128)(2,1)S(1)} %copy-done.5, s32[96,128]{1,0:T(8,128)S(1)} %copy-done, ...), custom_call_target="tpu_custom_call" | custom-call | tf_op jit(solution)/shard_map/forward/pallas_call | solution.py:303
  14.2 31.2 %all_to_all.10 = bf16[128,18,2,128]{3,2,1,0:T(2,128)(2,1)S(1)} all-to-all(bf16[128,18,2,128]{3,2,1,0:T(2,128)(2,1)S(1)} %bitcast.11), channel_id=1, replica_groups=mesh['ocn'=8,'lon'=16] {'ocn','lon'}, dimensions={0} | all-to-all | bytes 2359296 | tf_op jit(solution)/shard_map/all_to_all | solution.py:280
  45.5 0.0 copy-done.8
  45.5 0.0 copy-done.2
  45.5 5.8 %atmosphere.1 = (f32[6,50,128]{2,1,0:T(8,128)}, bf16[3840,128]{1,0:T(8,128)(2,1)S(1)}) custom-call(bf16[4608,128]{1,0:T(8,128)(2,1)S(1)} %bitcast.9, s32[5,1,128]{2,1,0:T(1,128)S(1)} %bitcast.16, f32[50,4,128]{2,1,0:T(4,128)S(1)} %bitcast.13), custom_call_target="tpu_custom_call" | custom-call | tf_op jit(solution)/shard_map/atmosphere/pallas_call | solution.py:328
  51.3 22.6 %all_to_all.11 = bf16[128,15,2,128]{3,2,1,0:T(2,128)(2,1)S(1)} all-to-all(bf16[128,15,2,128]{3,2,1,0:T(2,128)(2,1)S(1)} %bitcast.12), channel_id=1, replica_groups=mesh['ocn'=8,'lon'=16] {'ocn','lon'}, dimensions={0} | all-to-all | bytes 1966080 | tf_op jit(solution)/shard_map/all_to_all | solution.py:280
  73.9 0.0 copy-done.1
  74.0 6.5 %ocean.1 = f32[6,96,128]{2,1,0:T(8,128)} custom-call(bf16[3840,128]{1,0:T(8,128)(2,1)S(1)} %bitcast.10, bf16[640,128,128]{2,1,0:T(8,128)(2,1)S(1)} %get-tuple-element.9.kept, s32[672]{0:T(1024)S(1)} %get-tuple-element.10.list_hbm, s32[96,128]{1,0:T(8,128)S(1)} %copy-done.1), custom_call_target="tpu_custom_call" | custom-call | tf_op jit(solution)/shard_map/ocean/pallas_call | solution.py:348
Async XLA Ops:
  0.6 44.9 %copy-start.8 = (s32[1,128,5]{1,0,2:T(1,128)S(1)}, s32[1,128,5]{1,0,2:T(1,128)}, u32[]{:S(2)}) copy-start(s32[1,128,5]{1,0,2:T(1,128)} %param.16) | copy-start | bytes 7684
  0.6 0.8 %copy-start = (s32[96,128]{1,0:T(8,128)S(1)}, s32[96,128]{1,0:T(8,128)}, u32[]{:S(2)}) copy-start(s32[96,128]{1,0:T(8,128)} %mask.1) | copy-start | bytes 147460
  1.4 0.9 %copy-start.3 = (bf16[4,96,128]{2,1,0:T(8,128)(2,1)S(1)}, bf16[4,96,128]{2,1,0:T(8,128)(2,1)}, u32[]{:S(2)}) copy-start(bf16[4,96,128]{2,1,0:T(8,128)(2,1)} %state_hbm.1) | copy-start | bytes 294916
  2.3 0.7 copy-start.4
  3.1 0.7 copy-start.5
  3.8 0.7 copy-start.6
  4.5 0.7 copy-start.7
  5.2 40.3 %copy-start.2 = (f32[4,50,128]{2,0,1:T(4,128)S(1)}, f32[4,50,128]{2,0,1:T(4,128)}, u32[]{:S(2)}) copy-start(f32[4,50,128]{2,0,1:T(4,128)} %param.17) | copy-start | bytes 307204
  5.2 68.8 %copy-start.1 = (s32[96,128]{1,0:T(8,128)S(1)}, s32[96,128]{1,0:T(8,128)}, u32[]{:S(2)}) copy-start(s32[96,128]{1,0:T(8,128)} %mask.1) | copy-start | bytes 147460

commit v2 on v1

--- a/solution.py
+++ b/solution.py
@@ -8,17 +8,14 @@
 AXES = ("ocn", "lon")
 MB = 1024 * 1024
 
-PEER_BIT = 10
-TILE_BIT = 18
-GROUP = 16
+TILE_BIT = 10
+GROUP = 32
 CHUNKS = 16
 SUMS = 4
 
 
 def code_parts(code):
-    slot = code & ((1 << PEER_BIT) - 1)
-    peer = (code >> PEER_BIT) & ((1 << (TILE_BIT - PEER_BIT)) - 1)
-    return slot, peer, code >> TILE_BIT
+    return code & ((1 << TILE_BIT) - 1), code >> TILE_BIT
 
 
 def forward_kernel(
@@ -40,13 +37,13 @@
     target,
     fields,
     rows,
+    counts,
     sems,
     tile_sems,
 ):
     capacity, _, peers = target.shape
     slots = kept.shape[0]
     ocean_tiles = mask.shape[0]
-    per_chunk = slots // CHUNKS
     peers_chunk = peers // CHUNKS
     wire_rows = wire.shape[0]
     small = (
@@ -58,16 +55,33 @@
         (temp_hbm, temp),
     )
     copies = [pltpu.make_async_copy(a, b, sems.at[i]) for i, (a, b) in enumerate(small)]
-    for copy in copies:
+    for copy in copies[:2]:
         copy.start()
-
-    def chunk_copy(k):
-        part = pl.ds(k * per_chunk, per_chunk)
-        return pltpu.make_async_copy(tiles_hbm.at[part], kept.at[part], tile_sems.at[k])
-
-    for k in range(CHUNKS):
-        chunk_copy(k).start()
-    for copy in copies:
+    for copy in copies[2:]:
+        copy.start()
+    for copy in copies[:2]:
+        copy.wait()
+
+    def issue_chunk(k, carry):
+        count = jnp.int32(0)
+        for i in range(peers_chunk):
+            for c in range(capacity):
+                p = k * peers_chunk + i
+                slot = p * capacity + c
+                wanted = target[c, 0, p] >= 0
+
+                @pl.when(wanted)
+                def _():
+                    pltpu.make_async_copy(
+                        tiles_hbm.at[slot], kept.at[slot], tile_sems.at[k]
+                    ).start()
+
+                count = count + wanted.astype(jnp.int32)
+        counts[k] = count
+        return carry
+
+    lax.fori_loop(0, CHUNKS, issue_chunk, 0)
+    for copy in copies[2:]:
         copy.wait()
 
     sea = mask[...].astype(jnp.float32)
@@ -77,47 +91,41 @@
     fields[pl.ds(5, ocean_tiles, stride=8), :] = temp[...].astype(jnp.float32) * sea
     fields[pl.ds(6, ocean_tiles, stride=8), :] = sea
     fields[pl.ds(7, ocean_tiles, stride=8), :] = jnp.zeros_like(sea)
-    fields[8 * ocean_tiles :, :] = jnp.zeros((8, sea.shape[1]), jnp.float32)
-
-    def list_peer(p, count):
-        for c in range(capacity):
-            tile = source[c, 0, p]
-            listed[count] = (p * (capacity + (1 << PEER_BIT)) + c) + (tile << TILE_BIT)
-            count = count + (target[c, 0, p] >= 0).astype(jnp.int32)
+
+    def chunk(k, count):
+        arrived = counts[k]
+
+        @pl.when(arrived > 0)
+        def _():
+            part = pl.ds(0, arrived)
+            pltpu.make_async_copy(tiles_hbm.at[part], kept.at[part], tile_sems.at[k]).wait()
+
+        pairs = [(i, c) for i in range(peers_chunk) for c in range(capacity)]
+        for n in range(0, len(pairs), 2):
+            left, right, starts = [], [], []
+            for i, c in pairs[n : n + 2]:
+                p = k * peers_chunk + i
+                slot = p * capacity + c
+                tile = source[c, 0, p]
+                listed[count] = slot + (tile << TILE_BIT)
+                count = count + 1 + lax.shift_right_arithmetic(target[c, 0, p], 31)
+                left.append(fields[pl.ds(pl.multiple_of(tile * 8, 8), 8), :])
+                right.append(kept[slot])
+                starts.append(p * 36 + c * 7)
+            out = jnp.dot(
+                jnp.concatenate(left, 0).astype(jnp.bfloat16),
+                jnp.concatenate(right, 1),
+                preferred_element_type=jnp.float32,
+            )
+            rows[pl.ds(starts[0], 7), :] = out[0:7, 0:128]
+            rows[pl.ds(starts[1], 7), :] = out[8:15, 128:256]
         return count
 
-    count = lax.fori_loop(0, peers, list_peer, jnp.int32(0), unroll=4)
-    spare = (slots - 1) + ((wire_rows - 7 * (slots - 1)) << PEER_BIT) + (ocean_tiles << TILE_BIT)
+    count = lax.fori_loop(0, CHUNKS, chunk, jnp.int32(0))
+    spare = (slots - 1) + (ocean_tiles << TILE_BIT)
     for k in range(GROUP):
         listed[count + k] = spare
-    groups = (count + (GROUP - 1)) // GROUP
-    listed[slots + GROUP] = groups
-
-    def wait_chunk(k, carry):
-        chunk_copy(k).wait()
-        return carry
-
-    def group(g, waited):
-        parts = [code_parts(listed[g * GROUP + k]) for k in range(GROUP)]
-        need = jnp.minimum(parts[-1][1] // peers_chunk + 1, CHUNKS)
-        lax.fori_loop(waited, need, wait_chunk, 0)
-        for k in range(0, GROUP, 2):
-            (s0, p0, t0), (s1, p1, t1) = parts[k], parts[k + 1]
-            left = jnp.concatenate(
-                [
-                    fields[pl.ds(pl.multiple_of(t0 * 8, 8), 8), :],
-                    fields[pl.ds(pl.multiple_of(t1 * 8, 8), 8), :],
-                ],
-                0,
-            ).astype(jnp.bfloat16)
-            right = jnp.concatenate([kept[s0], kept[s1]], 1)
-            out = jnp.dot(left, right, preferred_element_type=jnp.float32)
-            rows[pl.ds(7 * s0 + p0, 7), :] = out[0:7, 0:128]
-            rows[pl.ds(7 * s1 + p1, 7), :] = out[8:15, 128:256]
-        return jnp.maximum(waited, need)
-
-    waited = lax.fori_loop(0, groups, group, jnp.int32(0))
-    lax.fori_loop(waited, CHUNKS, wait_chunk, 0)
+    listed[slots + GROUP] = (count + (GROUP - 1)) // GROUP
     step = wire_rows // 18
 
     def round_rows(i, carry):
@@ -129,7 +137,7 @@
 
 
 def atmosphere_kernel(
-    arrived, block_hbm, state, fluxes, wire, block, wide, sums, table, out_rows, sem
+    arrived, block_hbm, state, fluxes_hbm, wire, block, wide, fluxes, table, out_rows, sem, *sums
 ):
     capacity, _, peers = block.shape
     atm_tiles = state.shape[0]
@@ -144,8 +152,8 @@
         return carry
 
     lax.fori_loop(0, 18, widen, 0)
-    for c in range(capacity):
-        sums[c] = jnp.zeros(sums.shape[1:], jnp.float32)
+    for total in sums:
+        total[...] = jnp.zeros(total.shape, jnp.float32)
     copy.wait()
 
     def tile_of(p, c):
@@ -155,16 +163,16 @@
     def gather(p, carry):
         for c in range(capacity):
             part = pl.ds(tile_of(p, c), 8)
-            sums[c, part, :] = sums[c, part, :] + wide[pl.ds(p * 36 + c * 7, 8), :]
+            sums[c][part, :] = sums[c][part, :] + wide[pl.ds(p * 36 + c * 7, 8), :]
         return carry
 
     lax.fori_loop(0, peers, gather, 0, unroll=4)
     gathered = []
     for f in range(7):
         part = pl.ds(f, atm_tiles, stride=8)
-        total = sums[0, part, :]
+        total = sums[0][part, :]
         for c in range(1, capacity):
-            total = total + sums[c, part, :]
+            total = total + sums[c][part, :]
         gathered.append(total)
     inverse = 1.0 / jnp.maximum(gathered[6], 0.1)
     surface_temp, current_u, current_v, salinity, ice_frac, ice_surface = [
@@ -194,6 +202,8 @@
     for f, value in enumerate(results):
         fluxes[f] = value
         table[pl.ds(f, atm_tiles, stride=8), :] = value
+    flux_copy = pltpu.make_async_copy(fluxes, fluxes_hbm, sem)
+    flux_copy.start()
     table[8 * atm_tiles :, :] = jnp.zeros((8, value.shape[1]), jnp.float32)
 
     def send(p, carry):
@@ -210,9 +220,10 @@
         return carry
 
     lax.fori_loop(0, 16, round_rows, 0)
-
-
-def ocean_kernel(returned, kept, list_hbm, mask, out, listed, wide, sums, sem):
+    flux_copy.wait()
+
+
+def ocean_kernel(returned, kept, list_hbm, mask, out_hbm, listed, wide, out, sem, out_sems, *sums):
     slots = kept.shape[0]
     ocean_tiles = mask.shape[0]
     copy = pltpu.make_async_copy(list_hbm, listed, sem)
@@ -227,8 +238,8 @@
 
     lax.fori_loop(0, 16, widen, 0)
     wide[in_rows:, :] = jnp.zeros((8, wide.shape[1]), jnp.float32)
-    for k in range(SUMS):
-        sums[k] = jnp.zeros(sums.shape[1:], jnp.float32)
+    for total in sums:
+        total[...] = jnp.zeros(total.shape, jnp.float32)
     copy.wait()
     row = lax.broadcasted_iota(jnp.int32, (8, 128), 0)
 
@@ -236,7 +247,7 @@
         parts = [code_parts(listed[g * GROUP + k]) for k in range(GROUP)]
         for k in range(0, GROUP, 2):
             left = []
-            for slot, _, _ in parts[k : k + 2]:
+            for slot, _ in parts[k : k + 2]:
                 values = wide[pl.ds(6 * slot, 8), :]
                 left.append(jnp.where(row < 6, values, jnp.where(row == 6, 1.0, 0.0)))
             left = jnp.concatenate(left, 0).astype(jnp.bfloat16)
@@ -245,11 +256,11 @@
                 left, right, (((1,), (1,)), ((), ())), preferred_element_type=jnp.float32
             )
             for j in range(2):
-                tile = parts[k + j][2]
+                tile = parts[k + j][1]
                 part = pl.ds(pl.multiple_of(tile * 8, 8), 8)
-                n = (k + j) % SUMS
-                sums[n, part, :] = (
-                    sums[n, part, :] + terms[8 * j : 8 * j + 8, 128 * j : 128 * j + 128]
+                total = sums[(k + j) % SUMS]
+                total[part, :] = (
+                    total[part, :] + terms[8 * j : 8 * j + 8, 128 * j : 128 * j + 128]
                 )
         return carry
 
@@ -257,18 +268,27 @@
 
     def total(f):
         part = pl.ds(f, ocean_tiles, stride=8)
-        value = sums[0, part, :]
+        value = sums[0][part, :]
         for k in range(1, SUMS):
-            value = value + sums[k, part, :]
+            value = value + sums[k][part, :]
         return value
 
     scale = mask[...].astype(jnp.float32) / jnp.maximum(total(6), 0.1)
+    copies = []
     for f in range(6):
         out[f] = total(f) * scale
+        copies.append(pltpu.make_async_copy(out.at[f], out_hbm.at[f], out_sems.at[f]))
+        copies[-1].start()
+    for copy in copies:
+        copy.wait()
 
 
 def anywhere():
-    return pl.BlockSpec(memory_space=pl.ANY)
+    return pl.BlockSpec(memory_space=pltpu.HBM)
+
+
+def in_hbm(x):
+    return pltpu.with_memory_space_constraint(x, pltpu.HBM)
 
 
 def in_vmem():
@@ -300,6 +320,7 @@
     target = send_block.transpose(2, 0, 1)
     block = recv_block.transpose(2, 0, 1)
     list_size = slots + GROUP + 16
+    operands = (ocean_state, ice_cover, ice_temp, sea_mask, remap_tiles[0], source, target)
     kept, wire, listed = pl.pallas_call(
         forward_kernel,
         in_specs=[anywhere()] * 7,
@@ -316,19 +337,20 @@
             pltpu.VMEM(sea_mask.shape, jnp.int32),
             pltpu.SMEM(source.shape, jnp.int32),
             pltpu.SMEM(target.shape, jnp.int32),
-            pltpu.VMEM((8 * (ocean_tiles + 1), width), jnp.float32),
-            pltpu.VMEM((36 * peers + 8, width), jnp.float32),
+            pltpu.VMEM((8 * ocean_tiles, width), jnp.float32),
+            pltpu.VMEM((36 * peers, width), jnp.float32),
+            pltpu.SMEM((CHUNKS,), jnp.int32),
             pltpu.SemaphoreType.DMA((6,)),
             pltpu.SemaphoreType.DMA((CHUNKS,)),
         ],
         compiler_params=pltpu.CompilerParams(vmem_limit_bytes=16 * MB),
         name="forward",
-    )(ocean_state, ice_cover, ice_temp, sea_mask, remap_tiles[0], source, target)
+    )(*[in_hbm(x) for x in operands])
     arrived = exchange(wire, peers)
     fluxes, wire_back = pl.pallas_call(
         atmosphere_kernel,
-        in_specs=[in_vmem(), anywhere(), in_vmem()],
-        out_specs=[in_vmem(), in_vmem()],
+        in_specs=[in_vmem(), pl.BlockSpec(memory_space=pl.ANY), in_vmem()],
+        out_specs=[anywhere(), in_vmem()],
         out_shape=[
             jax.ShapeDtypeStruct((6, atm_tiles, width), jnp.float32),
             jax.ShapeDtypeStruct((30 * peers, width), jnp.bfloat16),
@@ -336,26 +358,29 @@
         scratch_shapes=[
             pltpu.SMEM(block.shape, jnp.int32),
             pltpu.VMEM((36 * peers + 8, width), jnp.float32),
-            pltpu.VMEM((capacity, 8 * (atm_tiles + 1), width), jnp.float32),
+            pltpu.VMEM((6, atm_tiles, width), jnp.float32),
             pltpu.VMEM((8 * (atm_tiles + 1), width), jnp.float32),
             pltpu.VMEM((30 * peers, width), jnp.float32),
             pltpu.SemaphoreType.DMA,
-        ],
+        ]
+        + [pltpu.VMEM((8 * (atm_tiles + 1), width), jnp.float32)] * capacity,
         compiler_params=pltpu.CompilerParams(vmem_limit_bytes=16 * MB),
         name="atmosphere",
     )(arrived, block, atm_state.transpose(1, 0, 2))
     returned = exchange(wire_back, peers)
     ocean_fluxes = pl.pallas_call(
         ocean_kernel,
-        in_specs=[in_vmem(), in_vmem(), anywhere(), in_vmem()],
-        out_specs=in_vmem(),
+        in_specs=[in_vmem(), in_vmem(), pl.BlockSpec(memory_space=pl.ANY), in_vmem()],
+        out_specs=anywhere(),
         out_shape=jax.ShapeDtypeStruct((6, ocean_tiles, width), jnp.float32),
         scratch_shapes=[
             pltpu.SMEM((list_size,), jnp.int32),
             pltpu.VMEM((30 * peers + 8, width), jnp.float32),
-            pltpu.VMEM((SUMS, 8 * (ocean_tiles + 1), width), jnp.float32),
+            pltpu.VMEM((6, ocean_tiles, width), jnp.float32),
             pltpu.SemaphoreType.DMA,
-        ],
+            pltpu.SemaphoreType.DMA((6,)),
+        ]
+        + [pltpu.VMEM((8 * (ocean_tiles + 1), width), jnp.float32)] * SUMS,
         compiler_params=pltpu.CompilerParams(vmem_limit_bytes=16 * MB),
         name="ocean",
     )(returned, kept, listed, sea_mask)

time: 80.9 us -> 72.6 us (0.90)
  local copies, waits for them, and re-layouts: 4.54 us -> 0.01 us
  Pallas kernels: 21.4 us -> 17.7 us
    unnamed x18 -> x6, local copies, waits for them, and re-layouts: 4.54 us -> 0.01 us
    pallas_call x2, Pallas kernels: 12.4 us -> 8.83 us  [the longest x1 5.08 us: shards(): pl.pallas_call(ocean_kernel, in_specs=[in_vmem(), in_vmem(), pl.BlockSpec...]
where the time goes in v2:
time: 72.6 us; the launch traced here: 72.4 us
  blocking collectives  54 us (74%)
  Pallas kernels  17.7 us (24%)
    all_to_all x2, blocking collectives, exchange(): lax.all_to_all(wire, AXES, split_axis=0, concat_axis=0, tiled=True)  54 us
    pallas_call x1, Pallas kernels, shards(): pl.pallas_call(forward_kernel, in_specs=[anywhere()] * 7, out_specs=[in_v...  8.89 us
    pallas_call x1, Pallas kernels, shards(): pl.pallas_call(ocean_kernel, in_specs=[in_vmem(), in_vmem(), pl.BlockSpec...  5.08 us
    pallas_call x1, Pallas kernels, shards(): pl.pallas_call(atmosphere_kernel, in_specs=[in_vmem(), pl.BlockSpec(memor...  3.76 us

profile of v2, /device:TPU:1, one launch (start us, length us, event | category | flops | bytes accessed | tf_op | source)
XLA Modules:
  0.0 72.4 jit_solution(9509476685052527560)
XLA Ops:
  0.6 0.0 copy-start
  0.6 0.0 copy-start.1
  0.7 0.0 copy-start.2
  0.7 8.9 %forward.1 = (bf16[640,128,128]{2,1,0:T(8,128)(2,1)S(1)}, bf16[4608,128]{1,0:T(8,128)(2,1)S(1)}, s32[688]{0:T(1024)S(1)}) custom-call(bf16[4,96,128]{2,1,0:T(8,128)(2,1)} %state_hbm.1, bf16[96,128]{1,0:T(8,128)(2,1)} %cover_hbm.1, bf16[96,128]{1,0:T(8,128)(2,1)} %temp_hbm.1, s32[96,128]{1,0:T(8,128)} %mask.1, bf16[640,128,128]{2,1,0:T(8,128)(2,1)} %bitcast.15, ...), custom_call_target="tpu_custom_call" | custom-call | tf_op jit(solution)/shard_map/forward/pallas_call | solution.py:324
  9.6 31.4 %all_to_all.10 = bf16[128,18,2,128]{3,2,1,0:T(2,128)(2,1)S(1)} all-to-all(bf16[128,18,2,128]{3,2,1,0:T(2,128)(2,1)S(1)} %bitcast.11), channel_id=1, replica_groups=mesh['ocn'=8,'lon'=16] {'ocn','lon'}, dimensions={0} | all-to-all | bytes 2359296 | tf_op jit(solution)/shard_map/all_to_all | solution.py:300
  41.0 0.0 copy-done.1
  41.0 0.0 copy-done.2
  41.0 3.8 %atmosphere.1 = (f32[6,50,128]{2,1,0:T(8,128)}, bf16[3840,128]{1,0:T(8,128)(2,1)S(1)}) custom-call(bf16[4608,128]{1,0:T(8,128)(2,1)S(1)} %bitcast.9, s32[5,1,128]{2,1,0:T(1,128)S(1)} %bitcast.14, f32[50,4,128]{2,1,0:T(4,128)S(1)} %bitcast.13), custom_call_target="tpu_custom_call" | custom-call | tf_op jit(solution)/shard_map/atmosphere/pallas_call | solution.py:350
  44.8 22.6 %all_to_all.11 = bf16[128,15,2,128]{3,2,1,0:T(2,128)(2,1)S(1)} all-to-all(bf16[128,15,2,128]{3,2,1,0:T(2,128)(2,1)S(1)} %bitcast.12), channel_id=1, replica_groups=mesh['ocn'=8,'lon'=16] {'ocn','lon'}, dimensions={0} | all-to-all | bytes 1966080 | tf_op jit(solution)/shard_map/all_to_all | solution.py:300
  67.4 0.0 copy-done
  67.4 5.1 %ocean.1 = f32[6,96,128]{2,1,0:T(8,128)} custom-call(bf16[3840,128]{1,0:T(8,128)(2,1)S(1)} %bitcast.10, bf16[640,128,128]{2,1,0:T(8,128)(2,1)S(1)} %get-tuple-element.9.kept, s32[688]{0:T(1024)S(1)} %get-tuple-element.10.list_hbm, s32[96,128]{1,0:T(8,128)S(1)} %copy-done), custom_call_target="tpu_custom_call" | custom-call | tf_op jit(solution)/shard_map/ocean/pallas_call | solution.py:371
Async XLA Ops:
  0.6 66.7 %copy-start = (s32[96,128]{1,0:T(8,128)S(1)}, s32[96,128]{1,0:T(8,128)}, u32[]{:S(2)}) copy-start(s32[96,128]{1,0:T(8,128)} %mask.1) | copy-start | bytes 147460
  0.6 40.3 %copy-start.1 = (f32[4,50,128]{2,0,1:T(4,128)S(1)}, f32[4,50,128]{2,0,1:T(4,128)}, u32[]{:S(2)}) copy-start(f32[4,50,128]{2,0,1:T(4,128)} %param.17) | copy-start | bytes 307204
  0.7 40.3 %copy-start.2 = (s32[1,128,5]{1,0,2:T(1,128)S(1)}, s32[1,128,5]{1,0,2:T(1,128)}, u32[]{:S(2)}) copy-start(s32[1,128,5]{1,0,2:T(1,128)} %param.16) | copy-start | bytes 7684

commit v3 on v2

--- a/solution.py
+++ b/solution.py
@@ -1,3 +1,5 @@
+import functools
+
 import jax
 import jax.numpy as jnp
 from jax import lax
@@ -8,17 +10,15 @@
 AXES = ("ocn", "lon")
 MB = 1024 * 1024
 
-TILE_BIT = 10
-GROUP = 32
-CHUNKS = 16
+GROUP = 104
+CHUNKS = 4
+WHOLE = 1
 SUMS = 4
-
-
-def code_parts(code):
-    return code & ((1 << TILE_BIT) - 1), code >> TILE_BIT
+PARTIAL = 10
 
 
 def forward_kernel(
+    atm_tiles,
     state_hbm,
     cover_hbm,
     temp_hbm,
@@ -26,15 +26,18 @@
     tiles_hbm,
     source_hbm,
     target_hbm,
+    block_hbm,
     kept,
     wire,
     listed,
+    place,
     state,
     cover,
     temp,
     mask,
     source,
     target,
+    block,
     fields,
     rows,
     counts,
@@ -42,7 +45,6 @@
     tile_sems,
 ):
     capacity, _, peers = target.shape
-    slots = kept.shape[0]
     ocean_tiles = mask.shape[0]
     peers_chunk = peers // CHUNKS
     wire_rows = wire.shape[0]
@@ -53,37 +55,54 @@
         (state_hbm, state),
         (cover_hbm, cover),
         (temp_hbm, temp),
+        (block_hbm, block),
     )
     copies = [pltpu.make_async_copy(a, b, sems.at[i]) for i, (a, b) in enumerate(small)]
     for copy in copies[:2]:
         copy.start()
     for copy in copies[2:]:
         copy.start()
+    per_chunk = peers_chunk * capacity
+    for k in range(WHOLE):
+        part = pl.ds(k * per_chunk, per_chunk)
+        pltpu.make_async_copy(tiles_hbm.at[part], kept.at[part], tile_sems.at[k]).start()
+        counts[k] = per_chunk
     for copy in copies[:2]:
         copy.wait()
 
-    def issue_chunk(k, carry):
-        count = jnp.int32(0)
-        for i in range(peers_chunk):
-            for c in range(capacity):
-                p = k * peers_chunk + i
-                slot = p * capacity + c
-                wanted = target[c, 0, p] >= 0
-
-                @pl.when(wanted)
-                def _():
-                    pltpu.make_async_copy(
-                        tiles_hbm.at[slot], kept.at[slot], tile_sems.at[k]
-                    ).start()
-
-                count = count + wanted.astype(jnp.int32)
-        counts[k] = count
-        return carry
-
-    lax.fori_loop(0, CHUNKS, issue_chunk, 0)
+    pairs = [(i, c) for i in range(peers_chunk) for c in range(capacity)]
+
+    def list_tile(k, i, c, count, fetch):
+        p = k * peers_chunk + i
+        slot = p * capacity + c
+        block_of = target[c, 0, p]
+        listed[count] = p + c * peers
+        if fetch:
+
+            @pl.when(block_of >= 0)
+            def _():
+                pltpu.make_async_copy(tiles_hbm.at[slot], kept.at[slot], tile_sems.at[k]).start()
+
+        return count + 1 + lax.shift_right_arithmetic(block_of, 31)
+
+    def issue(k, count):
+        first = count
+        for i, c in pairs:
+            count = list_tile(k, i, c, count, True)
+        counts[k] = count - first
+        return count
+
+    count = jnp.int32(0)
+    for k in range(WHOLE):
+        for i, c in pairs:
+            count = list_tile(k, i, c, count, False)
+    for k in range(WHOLE, CHUNKS):
+        count = issue(k, count)
+    listed[kept.shape[0]] = count
     for copy in copies[2:]:
         copy.wait()
 
+    place[...] = jnp.where(block[...] < 0, atm_tiles, block[...]) * 8
     sea = mask[...].astype(jnp.float32)
     for f in range(4):
         fields[pl.ds(f, ocean_tiles, stride=8), :] = state[f].astype(jnp.float32) * sea
@@ -92,26 +111,29 @@
     fields[pl.ds(6, ocean_tiles, stride=8), :] = sea
     fields[pl.ds(7, ocean_tiles, stride=8), :] = jnp.zeros_like(sea)
 
-    def chunk(k, count):
-        arrived = counts[k]
-
-        @pl.when(arrived > 0)
+    def wait_chunk(k, carry):
+        arriving = counts[k]
+
+        @pl.when(arriving > 0)
         def _():
-            part = pl.ds(0, arrived)
+            part = pl.ds(0, arriving)
             pltpu.make_async_copy(tiles_hbm.at[part], kept.at[part], tile_sems.at[k]).wait()
 
-        pairs = [(i, c) for i in range(peers_chunk) for c in range(capacity)]
-        for n in range(0, len(pairs), 2):
+        return carry
+
+    def group(g, waited):
+        codes = [listed[jnp.minimum(g * GROUP + k, count - 1)] for k in range(GROUP)]
+        need = (codes[-1] & (peers - 1)) // peers_chunk + 1
+        lax.fori_loop(waited, need, wait_chunk, 0)
+        for k in range(0, GROUP, 2):
             left, right, starts = [], [], []
-            for i, c in pairs[n : n + 2]:
-                p = k * peers_chunk + i
+            for code in codes[k : k + 2]:
+                p, c = code & (peers - 1), code >> (peers.bit_length() - 1)
                 slot = p * capacity + c
                 tile = source[c, 0, p]
-                listed[count] = slot + (tile << TILE_BIT)
-                count = count + 1 + lax.shift_right_arithmetic(target[c, 0, p], 31)
                 left.append(fields[pl.ds(pl.multiple_of(tile * 8, 8), 8), :])
                 right.append(kept[slot])
-                starts.append(p * 36 + c * 7)
+                starts.append(7 * slot + p)
             out = jnp.dot(
                 jnp.concatenate(left, 0).astype(jnp.bfloat16),
                 jnp.concatenate(right, 1),
@@ -119,13 +141,10 @@
             )
             rows[pl.ds(starts[0], 7), :] = out[0:7, 0:128]
             rows[pl.ds(starts[1], 7), :] = out[8:15, 128:256]
-        return count
-
-    count = lax.fori_loop(0, CHUNKS, chunk, jnp.int32(0))
-    spare = (slots - 1) + (ocean_tiles << TILE_BIT)
-    for k in range(GROUP):
-        listed[count + k] = spare
-    listed[slots + GROUP] = (count + (GROUP - 1)) // GROUP
+        return jnp.maximum(waited, need)
+
+    waited = lax.fori_loop(0, (count + (GROUP - 1)) // GROUP, group, jnp.int32(0))
+    lax.fori_loop(waited, CHUNKS, wait_chunk, 0)
     step = wire_rows // 18
 
     def round_rows(i, carry):
@@ -137,11 +156,11 @@
 
 
 def atmosphere_kernel(
-    arrived, block_hbm, state, fluxes_hbm, wire, block, wide, fluxes, table, out_rows, sem, *sums
+    arrived, place_hbm, state, fluxes_hbm, wire, place, wide, fluxes, table, out_rows, sem, *sums
 ):
-    capacity, _, peers = block.shape
+    capacity, _, peers = place.shape
     atm_tiles = state.shape[0]
-    copy = pltpu.make_async_copy(block_hbm, block, sem)
+    copy = pltpu.make_async_copy(place_hbm, place, sem)
     copy.start()
     in_rows = arrived.shape[0]
     step = in_rows // 18
@@ -157,22 +176,19 @@
     copy.wait()
 
     def tile_of(p, c):
-        b = block[c, 0, p]
-        return pl.multiple_of(jnp.where(b < 0, atm_tiles, b) * 8, 8)
-
-    def gather(p, carry):
+        return pl.multiple_of(place[c, 0, p], 8)
+
+    for p in range(peers):
         for c in range(capacity):
+            total = sums[(p * capacity + c) % PARTIAL]
             part = pl.ds(tile_of(p, c), 8)
-            sums[c][part, :] = sums[c][part, :] + wide[pl.ds(p * 36 + c * 7, 8), :]
-        return carry
-
-    lax.fori_loop(0, peers, gather, 0, unroll=4)
+            total[part, :] = total[part, :] + wide[p * 36 + c * 7 : p * 36 + c * 7 + 8, :]
     gathered = []
     for f in range(7):
         part = pl.ds(f, atm_tiles, stride=8)
         total = sums[0][part, :]
-        for c in range(1, capacity):
-            total = total + sums[c][part, :]
+        for partial in sums[1:]:
+            total = total + partial[part, :]
         gathered.append(total)
     inverse = 1.0 / jnp.maximum(gathered[6], 0.1)
     surface_temp, current_u, current_v, salinity, ice_frac, ice_surface = [
@@ -206,12 +222,10 @@
     flux_copy.start()
     table[8 * atm_tiles :, :] = jnp.zeros((8, value.shape[1]), jnp.float32)
 
-    def send(p, carry):
+    for p in range(peers):
         for c in range(capacity):
-            out_rows[pl.ds(p * 30 + c * 6, 6), :] = table[pl.ds(tile_of(p, c), 6), :]
-        return carry
-
-    lax.fori_loop(0, peers, send, 0, unroll=4)
+            start = p * 30 + c * 6
+            out_rows[start : start + 6, :] = table[pl.ds(tile_of(p, c), 6), :]
     back_step = wire.shape[0] // 16
 
     def round_rows(i, carry):
@@ -223,11 +237,29 @@
     flux_copy.wait()
 
 
-def ocean_kernel(returned, kept, list_hbm, mask, out_hbm, listed, wide, out, sem, out_sems, *sums):
-    slots = kept.shape[0]
+def ocean_kernel(
+    returned,
+    kept,
+    list_hbm,
+    source_hbm,
+    mask,
+    out_hbm,
+    listed,
+    source,
+    wide,
+    out,
+    sems,
+    out_sems,
+    *sums,
+):
+    capacity, _, peers = source.shape
     ocean_tiles = mask.shape[0]
-    copy = pltpu.make_async_copy(list_hbm, listed, sem)
-    copy.start()
+    copies = [
+        pltpu.make_async_copy(list_hbm, listed, sems.at[0]),
+        pltpu.make_async_copy(source_hbm, source, sems.at[1]),
+    ]
+    for copy in copies:
+        copy.start()
     in_rows = returned.shape[0]
     step = in_rows // 16
 
@@ -240,31 +272,37 @@
     wide[in_rows:, :] = jnp.zeros((8, wide.shape[1]), jnp.float32)
     for total in sums:
         total[...] = jnp.zeros(total.shape, jnp.float32)
-    copy.wait()
+    for copy in copies:
+        copy.wait()
     row = lax.broadcasted_iota(jnp.int32, (8, 128), 0)
+    filled = listed[kept.shape[0]]
 
     def group(g, carry):
-        parts = [code_parts(listed[g * GROUP + k]) for k in range(GROUP)]
         for k in range(0, GROUP, 2):
-            left = []
-            for slot, _ in parts[k : k + 2]:
+            left, right, parts = [], [], []
+            for n in (g * GROUP + k, g * GROUP + k + 1):
+                code = listed[jnp.minimum(n, filled - 1)]
+                p, c = code & (peers - 1), code >> (peers.bit_length() - 1)
+                slot = p * capacity + c
+                tile = jnp.where(n < filled, source[c, 0, p], ocean_tiles)
                 values = wide[pl.ds(6 * slot, 8), :]
                 left.append(jnp.where(row < 6, values, jnp.where(row == 6, 1.0, 0.0)))
-            left = jnp.concatenate(left, 0).astype(jnp.bfloat16)
-            right = jnp.concatenate([kept[parts[k][0]], kept[parts[k + 1][0]]], 0)
+                right.append(kept[slot])
+                parts.append(pl.ds(pl.multiple_of(tile * 8, 8), 8))
             terms = lax.dot_general(
-                left, right, (((1,), (1,)), ((), ())), preferred_element_type=jnp.float32
+                jnp.concatenate(left, 0).astype(jnp.bfloat16),
+                jnp.concatenate(right, 0),
+                (((1,), (1,)), ((), ())),
+                preferred_element_type=jnp.float32,
             )
-            for j in range(2):
-                tile = parts[k + j][1]
-                part = pl.ds(pl.multiple_of(tile * 8, 8), 8)
+            for j, part in enumerate(parts):
                 total = sums[(k + j) % SUMS]
                 total[part, :] = (
                     total[part, :] + terms[8 * j : 8 * j + 8, 128 * j : 128 * j + 128]
                 )
         return carry
 
-    lax.fori_loop(0, listed[slots + GROUP], group, 0)
+    lax.fori_loop(0, (filled + (GROUP - 1)) // GROUP, group, 0)
 
     def total(f):
         part = pl.ds(f, ocean_tiles, stride=8)
@@ -319,16 +357,25 @@
     source = source_tile.transpose(2, 0, 1)
     target = send_block.transpose(2, 0, 1)
     block = recv_block.transpose(2, 0, 1)
-    list_size = slots + GROUP + 16
-    operands = (ocean_state, ice_cover, ice_temp, sea_mask, remap_tiles[0], source, target)
-    kept, wire, listed = pl.pallas_call(
-        forward_kernel,
-        in_specs=[anywhere()] * 7,
-        out_specs=[in_vmem(), in_vmem(), pl.BlockSpec(memory_space=pltpu.SMEM)],
+    operands = (
+        ocean_state,
+        ice_cover,
+        ice_temp,
+        sea_mask,
+        remap_tiles[0],
+        source,
+        target,
+        block,
+    )
+    kept, wire, listed, place = pl.pallas_call(
+        functools.partial(forward_kernel, atm_tiles),
+        in_specs=[anywhere()] * 8,
+        out_specs=[in_vmem(), in_vmem(), pl.BlockSpec(memory_space=pltpu.SMEM), in_vmem()],
         out_shape=[
             pltpu.VMEM((slots, width, width), jnp.bfloat16),
             jax.ShapeDtypeStruct((36 * peers, width), jnp.bfloat16),
-            jax.ShapeDtypeStruct((list_size,), jnp.int32),
+            jax.ShapeDtypeStruct((slots + 8,), jnp.int32),
+            jax.ShapeDtypeStruct(block.shape, jnp.int32),
         ],
         scratch_shapes=[
             pltpu.VMEM(ocean_state.shape, jnp.bfloat16),
@@ -337,10 +384,11 @@
             pltpu.VMEM(sea_mask.shape, jnp.int32),
             pltpu.SMEM(source.shape, jnp.int32),
             pltpu.SMEM(target.shape, jnp.int32),
+            pltpu.VMEM(block.shape, jnp.int32),
             pltpu.VMEM((8 * ocean_tiles, width), jnp.float32),
             pltpu.VMEM((36 * peers, width), jnp.float32),
             pltpu.SMEM((CHUNKS,), jnp.int32),
-            pltpu.SemaphoreType.DMA((6,)),
+            pltpu.SemaphoreType.DMA((7,)),
             pltpu.SemaphoreType.DMA((CHUNKS,)),
         ],
         compiler_params=pltpu.CompilerParams(vmem_limit_bytes=16 * MB),
@@ -363,27 +411,28 @@
             pltpu.VMEM((30 * peers, width), jnp.float32),
             pltpu.SemaphoreType.DMA,
         ]
-        + [pltpu.VMEM((8 * (atm_tiles + 1), width), jnp.float32)] * capacity,
+        + [pltpu.VMEM((8 * (atm_tiles + 1), width), jnp.float32)] * PARTIAL,
         compiler_params=pltpu.CompilerParams(vmem_limit_bytes=16 * MB),
         name="atmosphere",
-    )(arrived, block, atm_state.transpose(1, 0, 2))
+    )(arrived, place, atm_state.transpose(1, 0, 2))
     returned = exchange(wire_back, peers)
     ocean_fluxes = pl.pallas_call(
         ocean_kernel,
-        in_specs=[in_vmem(), in_vmem(), pl.BlockSpec(memory_space=pl.ANY), in_vmem()],
+        in_specs=[in_vmem(), in_vmem(), pl.BlockSpec(memory_space=pl.ANY), anywhere(), in_vmem()],
         out_specs=anywhere(),
         out_shape=jax.ShapeDtypeStruct((6, ocean_tiles, width), jnp.float32),
         scratch_shapes=[
-            pltpu.SMEM((list_size,), jnp.int32),
+            pltpu.SMEM(listed.shape, jnp.int32),
+            pltpu.SMEM(source.shape, jnp.int32),
             pltpu.VMEM((30 * peers + 8, width), jnp.float32),
             pltpu.VMEM((6, ocean_tiles, width), jnp.float32),
-            pltpu.SemaphoreType.DMA,
+            pltpu.SemaphoreType.DMA((2,)),
             pltpu.SemaphoreType.DMA((6,)),
         ]
         + [pltpu.VMEM((8 * (ocean_tiles + 1), width), jnp.float32)] * SUMS,
         compiler_params=pltpu.CompilerParams(vmem_limit_bytes=16 * MB),
         name="ocean",
-    )(returned, kept, listed, sea_mask)
+    )(returned, kept, listed, in_hbm(source), sea_mask)
     return (ocean_fluxes, fluxes)
 
 

time: 72.6 us -> 69 us (0.950)
  Pallas kernels: 17.7 us -> 14.2 us
    pallas_call x1, Pallas kernels: 8.89 us -> 7.04 us  [shards(): pl.pallas_call(functools.partial(forward_kernel, atm_tiles), in_specs=[an...]
    pallas_call x1, Pallas kernels: 3.76 us -> 2.18 us  [shards(): pl.pallas_call(atmosphere_kernel, in_specs=[in_vmem(), pl.BlockSpec(memor...]
where the time goes in v3:
time: 69 us; the launch traced here: 68.8 us
  blocking collectives  53.9 us (78%)
  Pallas kernels  14.2 us (21%)
    all_to_all x2, blocking collectives, exchange(): lax.all_to_all(wire, AXES, split_axis=0, concat_axis=0, tiled=True)  53.9 us
    pallas_call x1, Pallas kernels, shards(): pl.pallas_call(functools.partial(forward_kernel, atm_tiles), in_specs=[an...  7.04 us
    pallas_call x1, Pallas kernels, shards(): pl.pallas_call(ocean_kernel, in_specs=[in_vmem(), in_vmem(), pl.BlockSpec...  4.95 us
    pallas_call x1, Pallas kernels, shards(): pl.pallas_call(atmosphere_kernel, in_specs=[in_vmem(), pl.BlockSpec(memor...  2.18 us

profile of v3, /device:TPU:1, one launch (start us, length us, event | category | flops | bytes accessed | tf_op | source)
XLA Modules:
  0.0 68.8 jit_solution(11029285071899612266)
XLA Ops:
  0.6 0.0 copy-start
  0.6 0.0 copy-start.1
  0.7 7.0 %forward.1 = (bf16[640,128,128]{2,1,0:T(8,128)(2,1)S(1)}, bf16[4608,128]{1,0:T(8,128)(2,1)S(1)}, s32[648]{0:T(1024)S(1)}, s32[5,1,128]{2,1,0:T(1,128)S(1)}) custom-call(bf16[4,96,128]{2,1,0:T(8,128)(2,1)} %state_hbm.1, bf16[96,128]{1,0:T(8,128)(2,1)} %cover_hbm.1, bf16[96,128]{1,0:T(8,128)(2,1)} %temp_hbm.1, s32[96,128]{1,0:T(8,128)} %mask.1, ...), custom_call_target="tpu_custom_call" | custom-call | tf_op jit(solution)/shard_map/forward/pallas_call | solution.py:370
  7.7 31.3 %all_to_all.10 = bf16[128,18,2,128]{3,2,1,0:T(2,128)(2,1)S(1)} all-to-all(bf16[128,18,2,128]{3,2,1,0:T(2,128)(2,1)S(1)} %bitcast.11), channel_id=1, replica_groups=mesh['ocn'=8,'lon'=16] {'ocn','lon'}, dimensions={0} | all-to-all | bytes 2359296 | tf_op jit(solution)/shard_map/all_to_all | solution.py:338
  39.0 0.0 copy-done.1
  39.0 2.2 %atmosphere.1 = (f32[6,50,128]{2,1,0:T(8,128)}, bf16[3840,128]{1,0:T(8,128)(2,1)S(1)}) custom-call(bf16[4608,128]{1,0:T(8,128)(2,1)S(1)} %bitcast.9, s32[5,1,128]{2,1,0:T(1,128)S(1)} %get-tuple-element.9.place_hbm, f32[50,4,128]{2,1,0:T(4,128)S(1)} %bitcast.13), custom_call_target="tpu_custom_call" | custom-call | tf_op jit(solution)/shard_map/atmosphere/pallas_call | solution.py:398
  41.2 22.6 %all_to_all.11 = bf16[128,15,2,128]{3,2,1,0:T(2,128)(2,1)S(1)} all-to-all(bf16[128,15,2,128]{3,2,1,0:T(2,128)(2,1)S(1)} %bitcast.12), channel_id=1, replica_groups=mesh['ocn'=8,'lon'=16] {'ocn','lon'}, dimensions={0} | all-to-all | bytes 1966080 | tf_op jit(solution)/shard_map/all_to_all | solution.py:338
  63.8 0.0 copy-done
  63.8 5.0 %ocean.1 = f32[6,96,128]{2,1,0:T(8,128)} custom-call(bf16[3840,128]{1,0:T(8,128)(2,1)S(1)} %bitcast.10, bf16[640,128,128]{2,1,0:T(8,128)(2,1)S(1)} %get-tuple-element.11.kept, s32[648]{0:T(1024)S(1)} %get-tuple-element.12.list_hbm, s32[5,1,128]{2,1,0:T(1,128)} %bitcast.16, s32[96,128]{1,0:T(8,128)S(1)} %copy-done), custom_call_target="tpu_custom_call" | custom-call | tf_op jit(solution)/shard_map/ocean/pallas_call | solution.py:419
Async XLA Ops:
  0.6 63.2 %copy-start = (s32[96,128]{1,0:T(8,128)S(1)}, s32[96,128]{1,0:T(8,128)}, u32[]{:S(2)}) copy-start(s32[96,128]{1,0:T(8,128)} %mask.1) | copy-start | bytes 147460
  0.6 38.4 %copy-start.1 = (f32[4,50,128]{2,0,1:T(4,128)S(1)}, f32[4,50,128]{2,0,1:T(4,128)}, u32[]{:S(2)}) copy-start(f32[4,50,128]{2,0,1:T(4,128)} %param.17) | copy-start | bytes 307204

commit v4 on v3

--- a/solution.py
+++ b/solution.py
@@ -11,7 +11,7 @@
 MB = 1024 * 1024
 
 GROUP = 104
-CHUNKS = 4
+CHUNKS = 8
 WHOLE = 1
 SUMS = 4
 PARTIAL = 10
@@ -29,7 +29,7 @@
     block_hbm,
     kept,
     wire,
-    listed,
+    listed_out,
     place,
     state,
     cover,
@@ -40,6 +40,7 @@
     block,
     fields,
     rows,
+    listed,
     counts,
     sems,
     tile_sems,
@@ -49,7 +50,6 @@
     peers_chunk = peers // CHUNKS
     wire_rows = wire.shape[0]
     small = (
-        (source_hbm, source),
         (target_hbm, target),
         (mask_hbm, mask),
         (state_hbm, state),
@@ -58,48 +58,48 @@
         (block_hbm, block),
     )
     copies = [pltpu.make_async_copy(a, b, sems.at[i]) for i, (a, b) in enumerate(small)]
-    for copy in copies[:2]:
-        copy.start()
-    for copy in copies[2:]:
+    copies += [
+        pltpu.make_async_copy(
+            source_hbm.at[c, 0], source.at[pl.ds(c * peers, peers)], sems.at[len(small) + c]
+        )
+        for c in range(capacity)
+    ]
+    for copy in copies:
         copy.start()
     per_chunk = peers_chunk * capacity
     for k in range(WHOLE):
         part = pl.ds(k * per_chunk, per_chunk)
         pltpu.make_async_copy(tiles_hbm.at[part], kept.at[part], tile_sems.at[k]).start()
         counts[k] = per_chunk
-    for copy in copies[:2]:
-        copy.wait()
+    copies[0].wait()
 
     pairs = [(i, c) for i in range(peers_chunk) for c in range(capacity)]
 
-    def list_tile(k, i, c, count, fetch):
-        p = k * peers_chunk + i
-        slot = p * capacity + c
-        block_of = target[c, 0, p]
-        listed[count] = p + c * peers
-        if fetch:
-
-            @pl.when(block_of >= 0)
+    for k in range(WHOLE, CHUNKS):
+        for i, c in pairs:
+            p = k * peers_chunk + i
+            slot = p * capacity + c
+
+            @pl.when(target[c, 0, p] >= 0)
             def _():
                 pltpu.make_async_copy(tiles_hbm.at[slot], kept.at[slot], tile_sems.at[k]).start()
 
-        return count + 1 + lax.shift_right_arithmetic(block_of, 31)
-
-    def issue(k, count):
-        first = count
-        for i, c in pairs:
-            count = list_tile(k, i, c, count, True)
-        counts[k] = count - first
-        return count
-
-    count = jnp.int32(0)
-    for k in range(WHOLE):
-        for i, c in pairs:
-            count = list_tile(k, i, c, count, False)
-    for k in range(WHOLE, CHUNKS):
-        count = issue(k, count)
-    listed[kept.shape[0]] = count
-    for copy in copies[2:]:
+    gaps = jnp.int32(0)
+    for k in range(CHUNKS):
+        first = gaps
+        for n, (i, c) in enumerate(pairs):
+            p = k * peers_chunk + i
+            listed[gaps + (k * per_chunk + n)] = p + c * peers
+            gaps = gaps + lax.shift_right_arithmetic(target[c, 0, p], 31)
+        if k >= WHOLE:
+            counts[k] = per_chunk + gaps - first
+    count = gaps + kept.shape[0]
+    for n in range(GROUP):
+        listed[count + n] = capacity * peers - 1
+    listed[kept.shape[0] + GROUP] = count
+    list_copy = pltpu.make_async_copy(listed, listed_out, sems.at[len(small) + capacity])
+    list_copy.start()
+    for copy in copies[1:]:
         copy.wait()
 
     place[...] = jnp.where(block[...] < 0, atm_tiles, block[...]) * 8
@@ -122,7 +122,7 @@
         return carry
 
     def group(g, waited):
-        codes = [listed[jnp.minimum(g * GROUP + k, count - 1)] for k in range(GROUP)]
+        codes = [listed[g * GROUP + k] for k in range(GROUP)]
         need = (codes[-1] & (peers - 1)) // peers_chunk + 1
         lax.fori_loop(waited, need, wait_chunk, 0)
         for k in range(0, GROUP, 2):
@@ -130,7 +130,7 @@
             for code in codes[k : k + 2]:
                 p, c = code & (peers - 1), code >> (peers.bit_length() - 1)
                 slot = p * capacity + c
-                tile = source[c, 0, p]
+                tile = source[code]
                 left.append(fields[pl.ds(pl.multiple_of(tile * 8, 8), 8), :])
                 right.append(kept[slot])
                 starts.append(7 * slot + p)
@@ -153,6 +153,7 @@
         return carry
 
     lax.fori_loop(0, 18, round_rows, 0)
+    list_copy.wait()
 
 
 def atmosphere_kernel(
@@ -241,7 +242,7 @@
     returned,
     kept,
     list_hbm,
-    source_hbm,
+    source_any,
     mask,
     out_hbm,
     listed,
@@ -252,11 +253,12 @@
     out_sems,
     *sums,
 ):
-    capacity, _, peers = source.shape
+    capacity, _, peers = source_any.shape
     ocean_tiles = mask.shape[0]
-    copies = [
-        pltpu.make_async_copy(list_hbm, listed, sems.at[0]),
-        pltpu.make_async_copy(source_hbm, source, sems.at[1]),
+    copies = [pltpu.make_async_copy(list_hbm, listed, sems.at[capacity])]
+    copies += [
+        pltpu.make_async_copy(source_any.at[c, 0], source.at[pl.ds(c * peers, peers)], sems.at[c])
+        for c in range(capacity)
     ]
     for copy in copies:
         copy.start()
@@ -275,16 +277,16 @@
     for copy in copies:
         copy.wait()
     row = lax.broadcasted_iota(jnp.int32, (8, 128), 0)
-    filled = listed[kept.shape[0]]
+    filled = listed[kept.shape[0] + GROUP]
 
     def group(g, carry):
         for k in range(0, GROUP, 2):
             left, right, parts = [], [], []
             for n in (g * GROUP + k, g * GROUP + k + 1):
-                code = listed[jnp.minimum(n, filled - 1)]
+                code = listed[n]
                 p, c = code & (peers - 1), code >> (peers.bit_length() - 1)
                 slot = p * capacity + c
-                tile = jnp.where(n < filled, source[c, 0, p], ocean_tiles)
+                tile = jnp.where(n < filled, source[code], ocean_tiles)
                 values = wide[pl.ds(6 * slot, 8), :]
                 left.append(jnp.where(row < 6, values, jnp.where(row == 6, 1.0, 0.0)))
                 right.append(kept[slot])
@@ -357,6 +359,7 @@
     source = source_tile.transpose(2, 0, 1)
     target = send_block.transpose(2, 0, 1)
     block = recv_block.transpose(2, 0, 1)
+    list_size = -(-(slots + GROUP + 1) // 128) * 128
     operands = (
         ocean_state,
         ice_cover,
@@ -370,11 +373,11 @@
     kept, wire, listed, place = pl.pallas_call(
         functools.partial(forward_kernel, atm_tiles),
         in_specs=[anywhere()] * 8,
-        out_specs=[in_vmem(), in_vmem(), pl.BlockSpec(memory_space=pltpu.SMEM), in_vmem()],
+        out_specs=[in_vmem(), in_vmem(), pl.BlockSpec(memory_space=pl.ANY), in_vmem()],
         out_shape=[
             pltpu.VMEM((slots, width, width), jnp.bfloat16),
             jax.ShapeDtypeStruct((36 * peers, width), jnp.bfloat16),
-            jax.ShapeDtypeStruct((slots + 8,), jnp.int32),
+            jax.ShapeDtypeStruct((list_size,), jnp.int32),
             jax.ShapeDtypeStruct(block.shape, jnp.int32),
         ],
         scratch_shapes=[
@@ -382,13 +385,14 @@
             pltpu.VMEM(ice_cover.shape, jnp.bfloat16),
             pltpu.VMEM(ice_temp.shape, jnp.bfloat16),
             pltpu.VMEM(sea_mask.shape, jnp.int32),
-            pltpu.SMEM(source.shape, jnp.int32),
+            pltpu.SMEM((slots,), jnp.int32),
             pltpu.SMEM(target.shape, jnp.int32),
             pltpu.VMEM(block.shape, jnp.int32),
             pltpu.VMEM((8 * ocean_tiles, width), jnp.float32),
             pltpu.VMEM((36 * peers, width), jnp.float32),
+            pltpu.SMEM((list_size,), jnp.int32),
             pltpu.SMEM((CHUNKS,), jnp.int32),
-            pltpu.SemaphoreType.DMA((7,)),
+            pltpu.SemaphoreType.DMA((7 + capacity,)),
             pltpu.SemaphoreType.DMA((CHUNKS,)),
         ],
         compiler_params=pltpu.CompilerParams(vmem_limit_bytes=16 * MB),
@@ -418,21 +422,21 @@
     returned = exchange(wire_back, peers)
     ocean_fluxes = pl.pallas_call(
         ocean_kernel,
-        in_specs=[in_vmem(), in_vmem(), pl.BlockSpec(memory_space=pl.ANY), anywhere(), in_vmem()],
+        in_specs=[in_vmem(), in_vmem()] + [pl.BlockSpec(memory_space=pl.ANY)] * 2 + [in_vmem()],
         out_specs=anywhere(),
         out_shape=jax.ShapeDtypeStruct((6, ocean_tiles, width), jnp.float32),
         scratch_shapes=[
             pltpu.SMEM(listed.shape, jnp.int32),
-            pltpu.SMEM(source.shape, jnp.int32),
+            pltpu.SMEM((slots,), jnp.int32),
             pltpu.VMEM((30 * peers + 8, width), jnp.float32),
             pltpu.VMEM((6, ocean_tiles, width), jnp.float32),
-            pltpu.SemaphoreType.DMA((2,)),
+            pltpu.SemaphoreType.DMA((1 + capacity,)),
             pltpu.SemaphoreType.DMA((6,)),
         ]
         + [pltpu.VMEM((8 * (ocean_tiles + 1), width), jnp.float32)] * SUMS,
         compiler_params=pltpu.CompilerParams(vmem_limit_bytes=16 * MB),
         name="ocean",
-    )(returned, kept, listed, in_hbm(source), sea_mask)
+    )(returned, kept, listed, source, sea_mask)
     return (ocean_fluxes, fluxes)
 
 

time: 69 us -> 67.6 us (0.980)
  Pallas kernels: 14.2 us -> 12.7 us
    pallas_call x1, Pallas kernels: 7.04 us -> 5.82 us  [shards(): pl.pallas_call(functools.partial(forward_kernel, atm_tiles), in_specs=[an...]
where the time goes in v4:
time: 67.6 us; the launch traced here: 67.4 us
  blocking collectives  54 us (80%)
  Pallas kernels  12.7 us (19%)
  between operations  0.68 us (1%)
    all_to_all x2, blocking collectives, exchange(): lax.all_to_all(wire, AXES, split_axis=0, concat_axis=0, tiled=True)  54 us
    pallas_call x1, Pallas kernels, shards(): pl.pallas_call(functools.partial(forward_kernel, atm_tiles), in_specs=[an...  5.82 us
    pallas_call x1, Pallas kernels, shards(): pl.pallas_call(ocean_kernel, in_specs=[in_vmem(), in_vmem()] + [pl.BlockS...  4.68 us
    pallas_call x1, Pallas kernels, shards(): pl.pallas_call(atmosphere_kernel, in_specs=[in_vmem(), pl.BlockSpec(memor...  2.18 us

profile of v4, /device:TPU:1, one launch (start us, length us, event | category | flops | bytes accessed | tf_op | source)
XLA Modules:
  0.0 67.4 jit_solution(9104087971209485542)
XLA Ops:
  0.6 0.0 copy-start
  0.6 0.0 copy-start.2
  0.7 0.0 copy-start.1
  0.7 5.8 %forward.1 = (bf16[640,128,128]{2,1,0:T(8,128)(2,1)S(1)}, bf16[4608,128]{1,0:T(8,128)(2,1)S(1)}, s32[768]{0:T(1024)S(1)}, s32[5,1,128]{2,1,0:T(1,128)S(1)}) custom-call(bf16[4,96,128]{2,1,0:T(8,128)(2,1)} %state_hbm.1, bf16[96,128]{1,0:T(8,128)(2,1)} %cover_hbm.1, bf16[96,128]{1,0:T(8,128)(2,1)} %temp_hbm.1, s32[96,128]{1,0:T(8,128)} %mask.1, ...), custom_call_target="tpu_custom_call" | custom-call | tf_op jit(solution)/shard_map/forward/pallas_call | solution.py:373
  6.5 31.4 %all_to_all.10 = bf16[128,18,2,128]{3,2,1,0:T(2,128)(2,1)S(1)} all-to-all(bf16[128,18,2,128]{3,2,1,0:T(2,128)(2,1)S(1)} %bitcast.11), channel_id=1, replica_groups=mesh['ocn'=8,'lon'=16] {'ocn','lon'}, dimensions={0} | all-to-all | bytes 2359296 | tf_op jit(solution)/shard_map/all_to_all | solution.py:340
  37.9 0.0 copy-done.1
  37.9 2.2 %atmosphere.1 = (f32[6,50,128]{2,1,0:T(8,128)}, bf16[3840,128]{1,0:T(8,128)(2,1)S(1)}) custom-call(bf16[4608,128]{1,0:T(8,128)(2,1)S(1)} %bitcast.9, s32[5,1,128]{2,1,0:T(1,128)S(1)} %get-tuple-element.9.place_hbm, f32[50,4,128]{2,1,0:T(4,128)S(1)} %bitcast.13), custom_call_target="tpu_custom_call" | custom-call | tf_op jit(solution)/shard_map/atmosphere/pallas_call | solution.py:402
  40.1 22.6 %all_to_all.11 = bf16[128,15,2,128]{3,2,1,0:T(2,128)(2,1)S(1)} all-to-all(bf16[128,15,2,128]{3,2,1,0:T(2,128)(2,1)S(1)} %bitcast.12), channel_id=1, replica_groups=mesh['ocn'=8,'lon'=16] {'ocn','lon'}, dimensions={0} | all-to-all | bytes 1966080 | tf_op jit(solution)/shard_map/all_to_all | solution.py:340
  62.7 0.0 copy-done
  62.7 0.0 copy-done.2
  62.7 4.7 %ocean.1 = f32[6,96,128]{2,1,0:T(8,128)} custom-call(bf16[3840,128]{1,0:T(8,128)(2,1)S(1)} %bitcast.10, bf16[640,128,128]{2,1,0:T(8,128)(2,1)S(1)} %get-tuple-element.11.kept, s32[768]{0:T(1024)S(1)} %get-tuple-element.12.list_hbm, s32[5,1,128]{2,1,0:T(1,128)S(1)} %bitcast.15, s32[96,128]{1,0:T(8,128)S(1)} %copy-done), custom_call_target="tpu_custom_call" | custom-call | tf_op jit(solution)/shard_map/ocean/pallas_call | solution.py:423
Async XLA Ops:
  0.6 62.1 %copy-start = (s32[96,128]{1,0:T(8,128)S(1)}, s32[96,128]{1,0:T(8,128)}, u32[]{:S(2)}) copy-start(s32[96,128]{1,0:T(8,128)} %mask.1) | copy-start | bytes 147460
  0.6 62.1 %copy-start.2 = (s32[1,128,5]{1,0,2:T(1,128)S(1)}, s32[1,128,5]{1,0,2:T(1,128)}, u32[]{:S(2)}) copy-start(s32[1,128,5]{1,0,2:T(1,128)} %param.14) | copy-start | bytes 7684
  0.7 37.3 %copy-start.1 = (f32[4,50,128]{2,0,1:T(4,128)S(1)}, f32[4,50,128]{2,0,1:T(4,128)}, u32[]{:S(2)}) copy-start(f32[4,50,128]{2,0,1:T(4,128)} %param.17) | copy-start | bytes 307204

commit v5 on v4

--- a/solution.py
+++ b/solution.py
@@ -13,7 +13,7 @@
 GROUP = 104
 CHUNKS = 8
 WHOLE = 1
-SUMS = 4
+SUMS = 2
 PARTIAL = 10
 
 
@@ -84,6 +84,18 @@
             def _():
                 pltpu.make_async_copy(tiles_hbm.at[slot], kept.at[slot], tile_sems.at[k]).start()
 
+    for copy in copies[1:]:
+        copy.wait()
+
+    place[...] = jnp.where(block[...] < 0, atm_tiles, block[...]) * 8
+    sea = mask[...].astype(jnp.float32)
+    for f in range(4):
+        fields[pl.ds(f, ocean_tiles, stride=8), :] = state[f].astype(jnp.float32) * sea
+    fields[pl.ds(4, ocean_tiles, stride=8), :] = cover[...].astype(jnp.float32) * sea
+    fields[pl.ds(5, ocean_tiles, stride=8), :] = temp[...].astype(jnp.float32) * sea
+    fields[pl.ds(6, ocean_tiles, stride=8), :] = sea
+    fields[pl.ds(7, ocean_tiles, stride=8), :] = jnp.zeros_like(sea)
+
     gaps = jnp.int32(0)
     for k in range(CHUNKS):
         first = gaps
@@ -99,17 +111,6 @@
     listed[kept.shape[0] + GROUP] = count
     list_copy = pltpu.make_async_copy(listed, listed_out, sems.at[len(small) + capacity])
     list_copy.start()
-    for copy in copies[1:]:
-        copy.wait()
-
-    place[...] = jnp.where(block[...] < 0, atm_tiles, block[...]) * 8
-    sea = mask[...].astype(jnp.float32)
-    for f in range(4):
-        fields[pl.ds(f, ocean_tiles, stride=8), :] = state[f].astype(jnp.float32) * sea
-    fields[pl.ds(4, ocean_tiles, stride=8), :] = cover[...].astype(jnp.float32) * sea
-    fields[pl.ds(5, ocean_tiles, stride=8), :] = temp[...].astype(jnp.float32) * sea
-    fields[pl.ds(6, ocean_tiles, stride=8), :] = sea
-    fields[pl.ds(7, ocean_tiles, stride=8), :] = jnp.zeros_like(sea)
 
     def wait_chunk(k, carry):
         arriving = counts[k]
@@ -184,13 +185,11 @@
             total = sums[(p * capacity + c) % PARTIAL]
             part = pl.ds(tile_of(p, c), 8)
             total[part, :] = total[part, :] + wide[p * 36 + c * 7 : p * 36 + c * 7 + 8, :]
-    gathered = []
-    for f in range(7):
-        part = pl.ds(f, atm_tiles, stride=8)
-        total = sums[0][part, :]
-        for partial in sums[1:]:
-            total = total + partial[part, :]
-        gathered.append(total)
+    together = sums[0][...]
+    for partial in sums[1:]:
+        together = together + partial[...]
+    table[...] = together
+    gathered = [table[pl.ds(f, atm_tiles, stride=8), :] for f in range(7)]
     inverse = 1.0 / jnp.maximum(gathered[6], 0.1)
     surface_temp, current_u, current_v, salinity, ice_frac, ice_surface = [
         g * inverse for g in gathered[:6]

time: 67.6 us -> 67.3 us (level)
  no operation moved by 1% of the time
where the time goes in v5:
time: 67.3 us; the launch traced here: 67.1 us
  blocking collectives  54.1 us (80%)
  Pallas kernels  12.4 us (18%)
  between operations  0.68 us (1%)
    all_to_all x2, blocking collectives, exchange(): lax.all_to_all(wire, AXES, split_axis=0, concat_axis=0, tiled=True)  54.1 us
    pallas_call x1, Pallas kernels, shards(): pl.pallas_call(functools.partial(forward_kernel, atm_tiles), in_specs=[an...  5.8 us
    pallas_call x1, Pallas kernels, shards(): pl.pallas_call(ocean_kernel, in_specs=[in_vmem(), in_vmem()] + [pl.BlockS...  4.55 us
    pallas_call x1, Pallas kernels, shards(): pl.pallas_call(atmosphere_kernel, in_specs=[in_vmem(), pl.BlockSpec(memor...  2.03 us

profile of v5, /device:TPU:1, one launch (start us, length us, event | category | flops | bytes accessed | tf_op | source)
XLA Modules:
  0.0 67.1 jit_solution(16108627522002944640)
XLA Ops:
  0.6 0.0 copy-start
  0.6 0.0 copy-start.2
  0.7 0.0 copy-start.1
  0.7 5.8 %forward.1 = (bf16[640,128,128]{2,1,0:T(8,128)(2,1)S(1)}, bf16[4608,128]{1,0:T(8,128)(2,1)S(1)}, s32[768]{0:T(1024)S(1)}, s32[5,1,128]{2,1,0:T(1,128)S(1)}) custom-call(bf16[4,96,128]{2,1,0:T(8,128)(2,1)} %state_hbm.1, bf16[96,128]{1,0:T(8,128)(2,1)} %cover_hbm.1, bf16[96,128]{1,0:T(8,128)(2,1)} %temp_hbm.1, s32[96,128]{1,0:T(8,128)} %mask.1, ...), custom_call_target="tpu_custom_call" | custom-call | tf_op jit(solution)/shard_map/forward/pallas_call | solution.py:372
  6.5 31.4 %all_to_all.10 = bf16[128,18,2,128]{3,2,1,0:T(2,128)(2,1)S(1)} all-to-all(bf16[128,18,2,128]{3,2,1,0:T(2,128)(2,1)S(1)} %bitcast.11), channel_id=1, replica_groups=mesh['ocn'=8,'lon'=16] {'ocn','lon'}, dimensions={0} | all-to-all | bytes 2359296 | tf_op jit(solution)/shard_map/all_to_all | solution.py:339
  37.9 0.0 copy-done.1
  37.9 2.0 %atmosphere.1 = (f32[6,50,128]{2,1,0:T(8,128)}, bf16[3840,128]{1,0:T(8,128)(2,1)S(1)}) custom-call(bf16[4608,128]{1,0:T(8,128)(2,1)S(1)} %bitcast.9, s32[5,1,128]{2,1,0:T(1,128)S(1)} %get-tuple-element.9.place_hbm, f32[50,4,128]{2,1,0:T(4,128)S(1)} %bitcast.13), custom_call_target="tpu_custom_call" | custom-call | tf_op jit(solution)/shard_map/atmosphere/pallas_call | solution.py:401
  40.0 22.6 %all_to_all.11 = bf16[128,15,2,128]{3,2,1,0:T(2,128)(2,1)S(1)} all-to-all(bf16[128,15,2,128]{3,2,1,0:T(2,128)(2,1)S(1)} %bitcast.12), channel_id=1, replica_groups=mesh['ocn'=8,'lon'=16] {'ocn','lon'}, dimensions={0} | all-to-all | bytes 1966080 | tf_op jit(solution)/shard_map/all_to_all | solution.py:339
  62.6 0.0 copy-done
  62.6 0.0 copy-done.2
  62.6 4.6 %ocean.1 = f32[6,96,128]{2,1,0:T(8,128)} custom-call(bf16[3840,128]{1,0:T(8,128)(2,1)S(1)} %bitcast.10, bf16[640,128,128]{2,1,0:T(8,128)(2,1)S(1)} %get-tuple-element.11.kept, s32[768]{0:T(1024)S(1)} %get-tuple-element.12.list_hbm, s32[5,1,128]{2,1,0:T(1,128)S(1)} %bitcast.15, s32[96,128]{1,0:T(8,128)S(1)} %copy-done), custom_call_target="tpu_custom_call" | custom-call | tf_op jit(solution)/shard_map/ocean/pallas_call | solution.py:422
Async XLA Ops:
  0.6 61.9 %copy-start = (s32[96,128]{1,0:T(8,128)S(1)}, s32[96,128]{1,0:T(8,128)}, u32[]{:S(2)}) copy-start(s32[96,128]{1,0:T(8,128)} %mask.1) | copy-start | bytes 147460
  0.6 61.9 %copy-start.2 = (s32[1,128,5]{1,0,2:T(1,128)S(1)}, s32[1,128,5]{1,0,2:T(1,128)}, u32[]{:S(2)}) copy-start(s32[1,128,5]{1,0,2:T(1,128)} %param.14) | copy-start | bytes 7684
  0.7 37.3 %copy-start.1 = (f32[4,50,128]{2,0,1:T(4,128)S(1)}, f32[4,50,128]{2,0,1:T(4,128)}, u32[]{:S(2)}) copy-start(f32[4,50,128]{2,0,1:T(4,128)} %param.17) | copy-start | bytes 307204
